TPU v7x, 512 devices: a whole 4x8x8 slice. The times are simulated.
512 devices in a mesh: scen: 64 (over z, y), fac: 8 (over x, core).
Axes of the slice: x: 4, y: 8, z: 8, core: 2. Of those that a mesh axis runs over, the one named last changes fastest.
Arguments:
- scenario_pnl: float32 [65536, 2048], P('scen', 'fac'), may hold values from -300 to 300
Outputs:
- covariance: float32 [2048, 2048], P('scen', 'fac')
- factor_means: float32 [2048], P('fac')
All inputs are finite; a program needn't handle non-finite values.
Results may differ from a plain program's by a relative error of at most 0.0003.
Values sent between devices are 32-bit elements; how exact they have to be, the bound alone decides.
No kernel may reach another device: no remote copies, remote signals or barrier semaphores. Data moves between devices by JAX's collectives and lax.ppermute only.
A program may use at most 64 MiB of HBM per device.

v0:
```python
import functools

import jax
import jax.numpy as jnp
from jax import lax
from jax.experimental import pallas as pl
from jax.experimental.pallas import tpu as pltpu
from jax.sharding import Mesh
from jax.sharding import PartitionSpec as P


SCEN = ("z1", "z0", "y1", "y0")
FAC = ("x", "c")
VMEM = pl.BlockSpec(memory_space=pltpu.VMEM)
F32 = jnp.float32
BF16 = jnp.bfloat16


def shape(*dims, dtype=F32):
    return jax.ShapeDtypeStruct(dims, dtype)


def outer(left, right):
    return lax.dot_general(
        left,
        right,
        (((0,), (0,)), ((), ())),
        precision=lax.Precision.HIGHEST,
        preferred_element_type=F32,
    )


def centre_kernel(x_ref, d_ref, a_ref, b_ref):
    rows, cols = x_ref.shape
    half = rows // 2
    mean = jnp.sum(x_ref[...], axis=0, keepdims=True) * (1.0 / rows)
    first, second = x_ref[0:half, :] - mean, x_ref[half:rows, :] - mean
    tail = jnp.broadcast_to(mean, (8, cols))
    d_ref[0:half, :] = first
    d_ref[half:rows, :] = second
    d_ref[rows : rows + 8, :] = tail
    a_ref[0:half, :] = first
    a_ref[half : half + 8, :] = tail
    b_ref[...] = second


def turn(piece, t_ref, at):
    cols = piece.shape[1]
    turned = piece.T
    high = turned.astype(BF16)
    t_ref[at : at + cols, :] = high
    t_ref[at + 2 * cols : at + 3 * cols, :] = (turned - high.astype(F32)).astype(BF16)


def against(t_ref, left, at, rows):
    high = left.astype(BF16)
    low = (left - high.astype(F32)).astype(BF16)
    two = t_ref.shape[0] // 2
    both = jnp.dot(t_ref[:, at : at + rows], high, preferred_element_type=F32)
    rest = jnp.dot(t_ref[0:two, at : at + rows], low, preferred_element_type=F32)
    return both[0:two] + (both[two:] + rest)


def deal(total, block, outs, at):
    cols = total.shape[1]
    y0, c = lax.axis_index("y0"), lax.axis_index("c")
    block[c] = total[0:cols].T.reshape(4, 2, 32, cols)
    block[1 - c] = total[cols:].T.reshape(4, 2, 32, cols)
    for dy in range(2):
        to = (1 - y0) if dy else y0
        for y1 in range(4):
            for j in range(2):
                lo = at + 32 * y1
                outs[dy][lo : lo + 32, cols * j : cols * j + cols] = block[j, y1, to]


def own_kernel(d_ref, s_ref, t_ref, *refs):
    outs, (block, mean) = refs[:2], refs[2:]
    cols = d_ref.shape[1]
    rows = d_ref.shape[0] - 8
    c = lax.axis_index("c")
    turn(d_ref[0:rows, :], t_ref, 0)
    turn(s_ref[0:rows, :], t_ref, cols)
    deal(against(t_ref, d_ref[0:rows, :], 0, rows), block, outs, 0)
    mean[c] = d_ref[rows : rows + 8, :]
    mean[1 - c] = s_ref[rows : rows + 8, :]
    for out in outs:
        out[128:136, :] = jnp.zeros((8, 2 * cols), F32)
        for j in range(2):
            out[128:129, cols * j : cols * j + cols] = mean[j, 0:1, :]
        out[129:130, 0:cols] = d_ref[rows : rows + 1, :]


def chips_kernel(n, t_ref, *refs):
    halves, outs, block = refs[: 2 * n], refs[2 * n : 2 * n + 2], refs[2 * n + 2]
    half, cols = halves[1].shape
    for k in range(n):
        a_ref, b_ref = halves[2 * k], halves[2 * k + 1]
        total = against(t_ref, a_ref[0:half, :], 0, half) + against(t_ref, b_ref[...], half, half)
        deal(total, block, outs, 128 * k)
    for out in outs:
        out[128 * n : 128 * n + 8, :] = jnp.zeros((8, 2 * cols), F32)
        for k in range(n):
            out[128 * n + k : 128 * n + k + 1, 0:cols] = halves[2 * k][half : half + 1, :]


def merge_pair_kernel(*refs):
    groups = [refs[3 * i : 3 * i + 3] for i in range(3)]
    keep_ref, send_ref, parts = refs[9:]
    cols = keep_ref.shape[1]
    z0, c = lax.axis_index("z0"), lax.axis_index("c")
    kept = jnp.full((1, 2 * cols), z0 == c)

    def read(group, lo, n):
        return jnp.where(kept, group[0][lo : lo + n, :], group[1][lo : lo + n, :]), group[2][lo : lo + n, :]

    def put(lo, value):
        n = value.shape[0]
        for j in range(2):
            parts[j, lo : lo + n, :] = value[:, cols * j : cols * j + cols]

    for group, n, at in zip(groups, (1, 2, 1), (0, 128, 384), strict=True):
        one, two = read(group, 0, 128 * n)
        put(at, one + two)
    put(512, jnp.zeros((16, 2 * cols), F32))
    own = read(groups[0], 128, 8)
    near = read(groups[1], 256, 8)
    far = read(groups[2], 128, 8)
    for dy in range(2):
        put(512 + dy, own[dy][0:1, :])
        for k, m in enumerate((own[dy][1:2, :], near[dy][0:1, :], near[dy][1:2, :], far[dy][0:1, :])):
            for j in range(2):
                parts[j, 514 + 2 * k + dy : 515 + 2 * k + dy, :] = m[:, 0:cols]
    keep_ref[...] = parts[c]
    send_ref[...] = parts[1 - c]


def merge_block_kernel(count, keep_ref, recv_ref, out_ref, shift):
    cols = keep_ref.shape[1]
    x, y0 = lax.axis_index("x"), lax.axis_index("y0")

    def centred(lo):
        means = jnp.concatenate([keep_ref[lo : lo + 2, :], recv_ref[lo : lo + 2, :]], axis=0)
        mean = jnp.sum(means, axis=0, keepdims=True) * 0.25
        return mean, jnp.concatenate([means - mean, jnp.zeros((4, cols), F32)], axis=0)

    own_mean, right = centred(512)
    for k, step in enumerate((0, 1, 3, 2)):
        mean, left = centred(514 + 2 * k)
        shift[...] = (outer(left, right) * float(count)).reshape(4, 2, 32, cols)
        to = lax.rem(x + step, 4)
        for y1 in range(4):
            lo = 128 * k + 32 * y1
            total = keep_ref[lo : lo + 32, :] + recv_ref[lo : lo + 32, :] + shift[y1, y0]
            out_ref[4 * to + y1, 0:32, :] = total
            out_ref[4 * to + y1, 32:33, :] = own_mean
            out_ref[4 * to + y1, 33:34, :] = mean
            out_ref[4 * to + y1, 34:40, :] = jnp.zeros((6, cols), F32)


def merge_all_kernel(count, in_ref, cov_ref, mean_ref, shift):
    blocks, _, cols = in_ref.shape
    total = in_ref[0, 0:32, :]
    for s in range(1, blocks):
        total = total + in_ref[s, 0:32, :]
    own = jnp.concatenate([in_ref[s, 32:33, :] for s in range(blocks)], axis=0)
    other = jnp.concatenate([in_ref[s, 33:34, :] for s in range(blocks)], axis=0)
    own_mean = jnp.sum(own, axis=0, keepdims=True) * (1.0 / blocks)
    other_mean = jnp.sum(other, axis=0, keepdims=True) * (1.0 / blocks)
    y = 2 * lax.axis_index("y1") + lax.axis_index("y0")
    shift[...] = (outer(other - other_mean, own - own_mean) * float(count)).reshape(8, 32, cols)
    cov_ref[...] = (total + shift[y]) / float(count * blocks - 1)
    mean_ref[...] = own_mean


def call(kernel, outs, args, scratch=(), mib=16, flops=0, moved=0):
    return pl.pallas_call(
        kernel,
        out_shape=outs,
        in_specs=[VMEM] * len(args),
        out_specs=jax.tree.map(lambda _: VMEM, outs),
        scratch_shapes=scratch,
        compiler_params=pltpu.CompilerParams(vmem_limit_bytes=mib * 2**20),
        cost_estimate=pl.CostEstimate(flops=flops, bytes_accessed=moved, transcendentals=0),
    )(*args)


def shifted(piece, axis, by):
    size = lax.axis_size(axis)
    return lax.ppermute(piece, axis, [(i, (i + by) % size) for i in range(size)])


def dealt(piece, dy):
    pairs = []
    for i in range(8):
        z0, y0, c = i // 4, i // 2 % 2, i % 2
        j = c * 4 + (y0 ^ dy) * 2 + z0
        if i != j:
            pairs.append((i, j))
    return lax.ppermute(piece, ("z0", "y0", "c"), pairs)


def steps(x):
    rows, cols = x.shape
    half = rows // 2
    d, a, b = call(
        centre_kernel,
        (shape(rows + 8, cols), shape(half + 8, cols), shape(half, cols)),
        (x,),
        flops=10**9,
        moved=2**21,
    )
    up_a = shifted(a, "x", -1)
    down_b = shifted(b, "x", 1)
    swap = shifted(d, "c", 1)
    block = pltpu.VMEM((2, 4, 2, 32, cols), F32)
    t, *own = call(
        own_kernel,
        (shape(4 * cols, rows, dtype=BF16), *[shape(136, 2 * cols)] * 2),
        (d, swap),
        (block, pltpu.VMEM((2, 8, cols), F32)),
        flops=2 * 10**9,
        moved=2**22,
    )
    a, b, *own = lax.optimization_barrier((a, b, *own))
    up_b = shifted(b, "x", -1)
    down_a = shifted(a, "x", 1)
    far_a = shifted(up_a, "x", -1)
    far_b = shifted(down_b, "x", 1)

    def gram(chips):
        n = len(chips) // 2
        return call(
            functools.partial(chips_kernel, n),
            [shape(128 * n + 8, 2 * cols)] * 2,
            (t, *chips),
            (block,),
            flops=2 * n * 10**9,
            moved=n * 2**21,
        )

    near = gram([up_a, up_b, down_a, down_b])
    far = gram([far_a, far_b])
    sums = []
    for outs in (own, near, far):
        sums += [outs[0]] + [dealt(outs[dy], dy) for dy in range(2)]
    keep, send = call(
        merge_pair_kernel,
        [shape(528, cols)] * 2,
        sums,
        (pltpu.VMEM((2, 528, cols), F32),),
        flops=10**9,
        moved=2**22,
    )
    merged = call(
        functools.partial(merge_block_kernel, rows),
        shape(16, 40, cols),
        (keep, shifted(send, "c", 1)),
        (pltpu.VMEM((4, 2, 32, cols), F32),),
        flops=10**9,
        moved=2**22,
    )
    merged = lax.all_to_all(merged, ("z1", "y1"), 0, 0, tiled=True)
    covariance, mean = call(
        functools.partial(merge_all_kernel, 4 * rows),
        (shape(32, cols), shape(1, cols)),
        (merged,),
        (pltpu.VMEM((8, 32, cols), F32),),
        flops=10**9,
        moved=2**20,
    )
    return covariance, mean.reshape(cols)


def solution(mesh):
    finer = Mesh(mesh.devices.reshape(4, 2, 4, 2, 4, 2), SCEN + FAC)
    return jax.shard_map(
        steps,
        mesh=finer,
        in_specs=(P(SCEN, FAC),),
        out_specs=(P(SCEN, FAC), P(FAC)),
        check_vma=False,
    )
```

profile of v0, /device:TPU:64, one launch (start us, length us, event | category | flops | bytes accessed | tf_op | source)
XLA Modules:
  0.0 114.8 jit_solution(11910655941417192675)
XLA Ops:
  0.6 1.2 %copy-done = f32[1024,256]{1,0:T(8,128)S(1)} copy-done((f32[1024,256]{1,0:T(8,128)S(1)}, f32[1024,256]{1,0:T(8,128)}, u32[]{:S(2)}) %copy-start) | copy-done | bytes 1048600
  2.1 1.9 %collective-permute-start = (f32[1032,256]{1,0:T(8,128)S(1)}, f32[1032,256]{1,0:T(8,128)S(1)}, u32[]{:S(2)}, u32[]{:S(2)}) collective-permute-start(f32[1032,256]{1,0:T(8,128)S(1)} %get-tuple-element.22.d_ref), channel_id=1, source_target_pairs={{0,1},{1,0},{2,3},{3,2},{4,5},{5,4},{6,7},{7,6},{8,9},{9,8},{10,11... | collective-permute-start | bytes 3170312 | tf_op jit(solution)/shard_map/ppermute | solution.py:190
  4.1 4.7 %collective-permute-start.3 = (f32[520,256]{1,0:T(8,128)S(1)}, f32[520,256]{1,0:T(8,128)S(1)}, u32[]{:S(2)}, u32[]{:S(2)}) collective-permute-start(f32[520,256]{1,0:T(8,128)S(1)} %get-tuple-element.29), channel_id=1, source_target_pairs={{0,6},{2,0},{4,2},{6,4},{1,7},{3,1},{5,3},{7,5},{8,14},{10,8},{12,... | collective-permute-start | bytes 1597448 | tf_op jit(solution)/shard_map/ppermute | solution.py:190
  8.8 1.9 %collective-permute-start.6 = (f32[512,256]{1,0:T(8,128)S(1)}, f32[512,256]{1,0:T(8,128)S(1)}, u32[]{:S(2)}, u32[]{:S(2)}) collective-permute-start(f32[512,256]{1,0:T(8,128)S(1)} %get-tuple-element.28), channel_id=1, source_target_pairs={{0,2},{2,4},{4,6},{6,0},{1,3},{3,5},{5,7},{7,1},{8,10},{10,12},{12... | collective-permute-start | bytes 1572872 | tf_op jit(solution)/shard_map/ppermute | solution.py:190
  10.7 1.3 %shard_map.31 = (bf16[1024,1024]{1,0:T(8,128)(2,1)S(1)}, f32[136,512]{1,0:T(8,128)S(1)}, f32[136,512]{1,0:T(8,128)S(1)}) custom-call(f32[1032,256]{1,0:T(8,128)S(1)} %get-tuple-element.22.d_ref, f32[1032,256]{1,0:T(8,128)S(1)} %collective-permute-done.s_ref), custom_call_target="tpu_custom_call" | custom-call | flops 2000000000 | bytes 4194304 | tf_op jit(solution)/shard_map/pallas_call | solution.py:177
  12.0 2.7 %collective-permute-start.5 = (f32[520,256]{1,0:T(8,128)S(1)}, f32[520,256]{1,0:T(8,128)S(1)}, u32[]{:S(2)}, u32[]{:S(2)}) collective-permute-start(f32[520,256]{1,0:T(8,128)S(1)} %get-tuple-element.29), channel_id=1, source_target_pairs={{0,2},{2,4},{4,6},{6,0},{1,3},{3,5},{5,7},{7,1},{8,10},{10,12},{12... | collective-permute-start | bytes 1597448 | tf_op jit(solution)/shard_map/ppermute | solution.py:190
  14.6 4.4 %collective-permute-start.4 = (f32[512,256]{1,0:T(8,128)S(1)}, f32[512,256]{1,0:T(8,128)S(1)}, u32[]{:S(2)}, u32[]{:S(2)}) collective-permute-start(f32[512,256]{1,0:T(8,128)S(1)} %get-tuple-element.28), channel_id=1, source_target_pairs={{0,6},{2,0},{4,2},{6,4},{1,7},{3,1},{5,3},{7,5},{8,14},{10,8},{12,... | collective-permute-start | bytes 1572872 | tf_op jit(solution)/shard_map/ppermute | solution.py:190
  19.0 2.2 %collective-permute-done.3.refs_0_ = f32[520,256]{1,0:T(8,128)S(1)} collective-permute-done((f32[520,256]{1,0:T(8,128)S(1)}, f32[520,256]{1,0:T(8,128)S(1)}, u32[]{:S(2)}, u32[]{:S(2)}) %collective-permute-start.3) | collective-permute-done | bytes 532512 | tf_op jit(solution)/shard_map/ppermute | solution.py:190
  21.2 5.6 %collective-permute-start.9 = (f32[520,256]{1,0:T(8,128)S(1)}, f32[520,256]{1,0:T(8,128)S(1)}, u32[]{:S(2)}, u32[]{:S(2)}) collective-permute-start(f32[520,256]{1,0:T(8,128)S(1)} %collective-permute-done.3.refs_0_), channel_id=1, source_target_pairs={{0,6},{2,0},{4,2},{6,4},{1,7},{3,1},{5,3},{7,5},{8,14},{10,8},{12,... | collective-permute-start | bytes 1597448 | tf_op jit(solution)/shard_map/ppermute | solution.py:190
  26.8 1.9 %collective-permute-start.10 = (f32[512,256]{1,0:T(8,128)S(1)}, f32[512,256]{1,0:T(8,128)S(1)}, u32[]{:S(2)}, u32[]{:S(2)}) collective-permute-start(f32[512,256]{1,0:T(8,128)S(1)} %collective-permute-done.6.refs_3_), channel_id=1, source_target_pairs={{0,2},{2,4},{4,6},{6,0},{1,3},{3,5},{5,7},{7,1},{8,10},{10,12},{12... | collective-permute-start | bytes 1572872 | tf_op jit(solution)/shard_map/ppermute | solution.py:190
  28.8 3.2 %collective-permute-start.1 = (f32[136,512]{1,0:T(8,128)S(1)}, f32[136,512]{1,0:T(8,128)S(1)}, u32[]{:S(2)}, u32[]{:S(2)}) collective-permute-start(f32[136,512]{1,0:T(8,128)S(1)} %get-tuple-element.25.refs_0_), channel_id=1, source_target_pairs={{1,64},{9,72},{64,1},{72,9},{3,66},{11,74},{66,3},{74,11},{5,68},{... | collective-permute-start | bytes 835592 | tf_op jit(solution)/shard_map/ppermute | solution.py:200
  32.5 5.6 %collective-permute-done.5.refs_2_ = f32[520,256]{1,0:T(8,128)S(1)} collective-permute-done((f32[520,256]{1,0:T(8,128)S(1)}, f32[520,256]{1,0:T(8,128)S(1)}, u32[]{:S(2)}, u32[]{:S(2)}) %collective-permute-start.5) | collective-permute-done | bytes 532512 | tf_op jit(solution)/shard_map/ppermute | solution.py:190
  38.1 2.1 %shard_map.32 = (f32[264,512]{1,0:T(8,128)S(1)}, f32[264,512]{1,0:T(8,128)S(1)}) custom-call(bf16[1024,1024]{1,0:T(8,128)(2,1)S(1)} %get-tuple-element.27.t_ref, f32[520,256]{1,0:T(8,128)S(1)} %collective-permute-done.3.refs_0_, f32[512,256]{1,0:T(8,128)S(1)} %collective-permute-done.4.refs_1_, f32[520,256]{1,0:T(8,128)S(1)} %collective-permute-done.5.refs_2_, ...), custom_call_target="tpu_custom_call" | custom-call | flops 4000000000 | bytes 4194304 | tf_op jit(solution)/shard_map/pallas_call | solution.py:177
  40.2 2.9 %collective-permute-start.7 = (f32[264,512]{1,0:T(8,128)S(1)}, f32[264,512]{1,0:T(8,128)S(1)}, u32[]{:S(2)}, u32[]{:S(2)}) collective-permute-start(f32[264,512]{1,0:T(8,128)S(1)} %get-tuple-element.30.refs_3_), channel_id=1, source_target_pairs={{1,64},{9,72},{64,1},{72,9},{3,66},{11,74},{66,3},{74,11},{5,68},{... | collective-permute-start | bytes 1622024 | tf_op jit(solution)/shard_map/ppermute | solution.py:200
  43.2 3.6 %collective-permute-start.8 = (f32[264,512]{1,0:T(8,128)S(1)}, f32[264,512]{1,0:T(8,128)S(1)}, u32[]{:S(2)}, u32[]{:S(2)}) collective-permute-start(f32[264,512]{1,0:T(8,128)S(1)} %get-tuple-element.31), channel_id=1, source_target_pairs={{0,8},{1,72},{8,0},{9,64},{64,9},{65,73},{72,1},{73,65},{2,10},{3,... | collective-permute-start | bytes 1622024 | tf_op jit(solution)/shard_map/ppermute | solution.py:200
  46.8 1.7 %collective-permute-done.10.refs_1_ = f32[512,256]{1,0:T(8,128)S(1)} collective-permute-done((f32[512,256]{1,0:T(8,128)S(1)}, f32[512,256]{1,0:T(8,128)S(1)}, u32[]{:S(2)}, u32[]{:S(2)}) %collective-permute-start.10) | collective-permute-done | bytes 524320 | tf_op jit(solution)/shard_map/ppermute | solution.py:190
  48.6 1.9 %collective-permute-start.2 = (f32[136,512]{1,0:T(8,128)S(1)}, f32[136,512]{1,0:T(8,128)S(1)}, u32[]{:S(2)}, u32[]{:S(2)}) collective-permute-start(f32[136,512]{1,0:T(8,128)S(1)} %get-tuple-element.26), channel_id=1, source_target_pairs={{0,8},{1,72},{8,0},{9,64},{64,9},{65,73},{72,1},{73,65},{2,10},{3,... | collective-permute-start | bytes 835592 | tf_op jit(solution)/shard_map/ppermute | solution.py:200
  51.6 4.7 %collective-permute-start.11 = (f32[136,512]{1,0:T(8,128)S(1)}, f32[136,512]{1,0:T(8,128)S(1)}, u32[]{:S(2)}, u32[]{:S(2)}) collective-permute-start(f32[136,512]{1,0:T(8,128)S(1)} %get-tuple-element.32.refs_6_), channel_id=1, source_target_pairs={{1,64},{9,72},{64,1},{72,9},{3,66},{11,74},{66,3},{74,11},{5,68},{... | collective-permute-start | bytes 835592 | tf_op jit(solution)/shard_map/ppermute | solution.py:200
  56.3 3.6 %collective-permute-start.12 = (f32[136,512]{1,0:T(8,128)S(1)}, f32[136,512]{1,0:T(8,128)S(1)}, u32[]{:S(2)}, u32[]{:S(2)}) collective-permute-start(f32[136,512]{1,0:T(8,128)S(1)} %get-tuple-element.33), channel_id=1, source_target_pairs={{0,8},{1,72},{8,0},{9,64},{64,9},{65,73},{72,1},{73,65},{2,10},{3,... | collective-permute-start | bytes 835592 | tf_op jit(solution)/shard_map/ppermute | solution.py:200
  59.9 6.7 %collective-permute-done.2.refs_2_ = f32[136,512]{1,0:T(8,128)S(1)} collective-permute-done((f32[136,512]{1,0:T(8,128)S(1)}, f32[136,512]{1,0:T(8,128)S(1)}, u32[]{:S(2)}, u32[]{:S(2)}) %collective-permute-start.2) | collective-permute-done | bytes 278560 | tf_op jit(solution)/shard_map/ppermute | solution.py:200
  66.5 5.1 %collective-permute-done.12.refs_8_ = f32[136,512]{1,0:T(8,128)S(1)} collective-permute-done((f32[136,512]{1,0:T(8,128)S(1)}, f32[136,512]{1,0:T(8,128)S(1)}, u32[]{:S(2)}, u32[]{:S(2)}) %collective-permute-start.12) | collective-permute-done | bytes 278560 | tf_op jit(solution)/shard_map/ppermute | solution.py:200
  71.9 1.9 %collective-permute-start.13 = (f32[528,256]{1,0:T(8,128)S(1)}, f32[528,256]{1,0:T(8,128)S(1)}, u32[]{:S(2)}, u32[]{:S(2)}) collective-permute-start(f32[528,256]{1,0:T(8,128)S(1)} %get-tuple-element.35), channel_id=1, source_target_pairs={{0,1},{1,0},{2,3},{3,2},{4,5},{5,4},{6,7},{7,6},{8,9},{9,8},{10,11... | collective-permute-start | bytes 1622024 | tf_op jit(solution)/shard_map/ppermute | solution.py:190
  73.8 1.9 %collective-permute-done.13.recv_ref = f32[528,256]{1,0:T(8,128)S(1)} collective-permute-done((f32[528,256]{1,0:T(8,128)S(1)}, f32[528,256]{1,0:T(8,128)S(1)}, u32[]{:S(2)}, u32[]{:S(2)}) %collective-permute-start.13) | collective-permute-done | bytes 540704 | tf_op jit(solution)/shard_map/ppermute | solution.py:190
  76.9 36.8 %all_to_all.5.in_ref = f32[16,40,256]{2,1,0:T(8,128)S(1)} all-to-all(f32[16,40,256]{2,1,0:T(8,128)S(1)} %shard_map.35), channel_id=1, replica_groups=mesh['z1'=4,'z0'=2,'y1'=4,'y0'=2,'x'=4,'c'=2] {'z1','y1'}, dimensions={0} | all-to-all | bytes 1310720 | tf_op jit(solution)/shard_map/all_to_all | solution.py:263
  (14 shorter events, 4.5 us)
Async XLA Ops:
  0.6 1.2 %copy-start = (f32[1024,256]{1,0:T(8,128)S(1)}, f32[1024,256]{1,0:T(8,128)}, u32[]{:S(2)}) copy-start(f32[1024,256]{1,0:T(8,128)} %x_ref.1) | copy-start | bytes 3145732
  2.1 8.5 %collective-permute-start = (f32[1032,256]{1,0:T(8,128)S(1)}, f32[1032,256]{1,0:T(8,128)S(1)}, u32[]{:S(2)}, u32[]{:S(2)}) collective-permute-start(f32[1032,256]{1,0:T(8,128)S(1)} %get-tuple-element.22.d_ref), channel_id=1, source_target_pairs={{0,1},{1,0},{2,3},{3,2},{4,5},{5,4},{6,7},{7,6},{8,9},{9,8},{10,11... | collective-permute-start | bytes 3170312 | tf_op jit(solution)/shard_map/ppermute | solution.py:190
  4.1 17.1 %collective-permute-start.3 = (f32[520,256]{1,0:T(8,128)S(1)}, f32[520,256]{1,0:T(8,128)S(1)}, u32[]{:S(2)}, u32[]{:S(2)}) collective-permute-start(f32[520,256]{1,0:T(8,128)S(1)} %get-tuple-element.29), channel_id=1, source_target_pairs={{0,6},{2,0},{4,2},{6,4},{1,7},{3,1},{5,3},{7,5},{8,14},{10,8},{12,... | collective-permute-start | bytes 1597448 | tf_op jit(solution)/shard_map/ppermute | solution.py:190
  8.8 18.1 %collective-permute-start.6 = (f32[512,256]{1,0:T(8,128)S(1)}, f32[512,256]{1,0:T(8,128)S(1)}, u32[]{:S(2)}, u32[]{:S(2)}) collective-permute-start(f32[512,256]{1,0:T(8,128)S(1)} %get-tuple-element.28), channel_id=1, source_target_pairs={{0,2},{2,4},{4,6},{6,0},{1,3},{3,5},{5,7},{7,1},{8,10},{10,12},{12... | collective-permute-start | bytes 1572872 | tf_op jit(solution)/shard_map/ppermute | solution.py:190
  12.0 26.1 %collective-permute-start.5 = (f32[520,256]{1,0:T(8,128)S(1)}, f32[520,256]{1,0:T(8,128)S(1)}, u32[]{:S(2)}, u32[]{:S(2)}) collective-permute-start(f32[520,256]{1,0:T(8,128)S(1)} %get-tuple-element.29), channel_id=1, source_target_pairs={{0,2},{2,4},{4,6},{6,0},{1,3},{3,5},{5,7},{7,1},{8,10},{10,12},{12... | collective-permute-start | bytes 1597448 | tf_op jit(solution)/shard_map/ppermute | solution.py:190
  14.6 17.8 %collective-permute-start.4 = (f32[512,256]{1,0:T(8,128)S(1)}, f32[512,256]{1,0:T(8,128)S(1)}, u32[]{:S(2)}, u32[]{:S(2)}) collective-permute-start(f32[512,256]{1,0:T(8,128)S(1)} %get-tuple-element.28), channel_id=1, source_target_pairs={{0,6},{2,0},{4,2},{6,4},{1,7},{3,1},{5,3},{7,5},{8,14},{10,8},{12,... | collective-permute-start | bytes 1572872 | tf_op jit(solution)/shard_map/ppermute | solution.py:190
  21.2 29.2 %collective-permute-start.9 = (f32[520,256]{1,0:T(8,128)S(1)}, f32[520,256]{1,0:T(8,128)S(1)}, u32[]{:S(2)}, u32[]{:S(2)}) collective-permute-start(f32[520,256]{1,0:T(8,128)S(1)} %collective-permute-done.3.refs_0_), channel_id=1, source_target_pairs={{0,6},{2,0},{4,2},{6,4},{1,7},{3,1},{5,3},{7,5},{8,14},{10,8},{12,... | collective-permute-start | bytes 1597448 | tf_op jit(solution)/shard_map/ppermute | solution.py:190
  26.8 21.7 %collective-permute-start.10 = (f32[512,256]{1,0:T(8,128)S(1)}, f32[512,256]{1,0:T(8,128)S(1)}, u32[]{:S(2)}, u32[]{:S(2)}) collective-permute-start(f32[512,256]{1,0:T(8,128)S(1)} %collective-permute-done.6.refs_3_), channel_id=1, source_target_pairs={{0,2},{2,4},{4,6},{6,0},{1,3},{3,5},{5,7},{7,1},{8,10},{10,12},{12... | collective-permute-start | bytes 1572872 | tf_op jit(solution)/shard_map/ppermute | solution.py:190
  28.8 27.5 %collective-permute-start.1 = (f32[136,512]{1,0:T(8,128)S(1)}, f32[136,512]{1,0:T(8,128)S(1)}, u32[]{:S(2)}, u32[]{:S(2)}) collective-permute-start(f32[136,512]{1,0:T(8,128)S(1)} %get-tuple-element.25.refs_0_), channel_id=1, source_target_pairs={{1,64},{9,72},{64,1},{72,9},{3,66},{11,74},{66,3},{74,11},{5,68},{... | collective-permute-start | bytes 835592 | tf_op jit(solution)/shard_map/ppermute | solution.py:200
  40.2 31.4 %collective-permute-start.7 = (f32[264,512]{1,0:T(8,128)S(1)}, f32[264,512]{1,0:T(8,128)S(1)}, u32[]{:S(2)}, u32[]{:S(2)}) collective-permute-start(f32[264,512]{1,0:T(8,128)S(1)} %get-tuple-element.30.refs_3_), channel_id=1, source_target_pairs={{1,64},{9,72},{64,1},{72,9},{3,66},{11,74},{66,3},{74,11},{5,68},{... | collective-permute-start | bytes 1622024 | tf_op jit(solution)/shard_map/ppermute | solution.py:200
  43.2 28.4 %collective-permute-start.8 = (f32[264,512]{1,0:T(8,128)S(1)}, f32[264,512]{1,0:T(8,128)S(1)}, u32[]{:S(2)}, u32[]{:S(2)}) collective-permute-start(f32[264,512]{1,0:T(8,128)S(1)} %get-tuple-element.31), channel_id=1, source_target_pairs={{0,8},{1,72},{8,0},{9,64},{64,9},{65,73},{72,1},{73,65},{2,10},{3,... | collective-permute-start | bytes 1622024 | tf_op jit(solution)/shard_map/ppermute | solution.py:200
  48.6 18.0 %collective-permute-start.2 = (f32[136,512]{1,0:T(8,128)S(1)}, f32[136,512]{1,0:T(8,128)S(1)}, u32[]{:S(2)}, u32[]{:S(2)}) collective-permute-start(f32[136,512]{1,0:T(8,128)S(1)} %get-tuple-element.26), channel_id=1, source_target_pairs={{0,8},{1,72},{8,0},{9,64},{64,9},{65,73},{72,1},{73,65},{2,10},{3,... | collective-permute-start | bytes 835592 | tf_op jit(solution)/shard_map/ppermute | solution.py:200
  51.6 14.9 %collective-permute-start.11 = (f32[136,512]{1,0:T(8,128)S(1)}, f32[136,512]{1,0:T(8,128)S(1)}, u32[]{:S(2)}, u32[]{:S(2)}) collective-permute-start(f32[136,512]{1,0:T(8,128)S(1)} %get-tuple-element.32.refs_6_), channel_id=1, source_target_pairs={{1,64},{9,72},{64,1},{72,9},{3,66},{11,74},{66,3},{74,11},{5,68},{... | collective-permute-start | bytes 835592 | tf_op jit(solution)/shard_map/ppermute | solution.py:200
  56.3 15.3 %collective-permute-start.12 = (f32[136,512]{1,0:T(8,128)S(1)}, f32[136,512]{1,0:T(8,128)S(1)}, u32[]{:S(2)}, u32[]{:S(2)}) collective-permute-start(f32[136,512]{1,0:T(8,128)S(1)} %get-tuple-element.33), channel_id=1, source_target_pairs={{0,8},{1,72},{8,0},{9,64},{64,9},{65,73},{72,1},{73,65},{2,10},{3,... | collective-permute-start | bytes 835592 | tf_op jit(solution)/shard_map/ppermute | solution.py:200
  71.9 3.8 %collective-permute-start.13 = (f32[528,256]{1,0:T(8,128)S(1)}, f32[528,256]{1,0:T(8,128)S(1)}, u32[]{:S(2)}, u32[]{:S(2)}) collective-permute-start(f32[528,256]{1,0:T(8,128)S(1)} %get-tuple-element.35), channel_id=1, source_target_pairs={{0,1},{1,0},{2,3},{3,2},{4,5},{5,4},{6,7},{7,6},{8,9},{9,8},{10,11... | collective-permute-start | bytes 1622024 | tf_op jit(solution)/shard_map/ppermute | solution.py:190
where the time goes:
time: 115 us
  starting transfers between devices  44.9 us (39%)
  blocking collectives  36.8 us (32%)
  waiting for transfers between devices  23.7 us (21%)
  Pallas kernels  7.36 us (6%)
  local copies, waits for them, and re-layouts  1.22 us (1%)
    all_to_all x1, blocking collectives, steps(): merged = lax.all_to_all(merged, ('z1', 'y1'), 0, 0, tiled=True)  36.8 us
    ppermute x8, starting transfers between devices, shifted(): lax.ppermute(piece, axis, [(i, (i + by) % size) for i in range(size)])  25 us
    ppermute x6, starting transfers between devices, dealt(): return lax.ppermute(piece, ('z0', 'y0', 'c'), pairs)  19.9 us
    ppermute x8, waiting for transfers between devices, shifted(): lax.ppermute(piece, axis, [(i, (i + by) % size) for i in range(size)])  11.9 us
    ppermute x6, waiting for transfers between devices, dealt(): return lax.ppermute(piece, ('z0', 'y0', 'c'), pairs)  11.7 us
    pallas_call x7, Pallas kernels, call(): pl.pallas_call(kernel, out_shape=outs, in_specs=[VMEM] * len(args), out_s...  7.36 us
  transfers between devices with their start and end apart: 14, of which 7 were waited for; matrix products, arithmetic and copies ran while one was open for 0% of the time, Pallas kernels for 4%

commit v1 on v0

v1 whole, which is shorter than its diff:
```python
import functools

import jax
import jax.numpy as jnp
from jax import lax
from jax.experimental import pallas as pl
from jax.experimental.pallas import tpu as pltpu
from jax.sharding import Mesh
from jax.sharding import PartitionSpec as P


SCEN = ("z1", "z0", "y1", "y0")
FAC = ("x", "c")
VMEM = pl.BlockSpec(memory_space=pltpu.VMEM)
F32 = jnp.float32
BF16 = jnp.bfloat16


def shape(*dims, dtype=F32):
    return jax.ShapeDtypeStruct(dims, dtype)


def outer(left, right):
    return lax.dot_general(
        left,
        right,
        (((0,), (0,)), ((), ())),
        precision=lax.Precision.HIGHEST,
        preferred_element_type=F32,
    )


def centre_kernel(x_ref, d_ref):
    rows, cols = x_ref.shape
    mean = jnp.sum(x_ref[...], axis=0, keepdims=True) * (1.0 / rows)
    d_ref[0:rows, :] = x_ref[...] - mean
    d_ref[rows : rows + 8, :] = jnp.broadcast_to(mean, (8, cols))


def turn(piece, t_ref, at):
    cols = piece.shape[1]
    high, low = split(piece.T)
    t_ref[at : at + cols, :] = high
    t_ref[at + 2 * cols : at + 3 * cols, :] = low


def split(value):
    high = value.astype(BF16)
    return high, (value - high.astype(F32)).astype(BF16)


def against(t_ref, left):
    high, low = split(left)
    two = t_ref.shape[0] // 2
    both = jnp.dot(t_ref[...], high, preferred_element_type=F32)
    rest = jnp.dot(t_ref[0:two, :], low, preferred_element_type=F32)
    return both[0:two] + (both[two:] + rest)


def deal(total, block, outs, at):
    cols = total.shape[1]
    y0, c = lax.axis_index("y0"), lax.axis_index("c")
    block[c] = total[0:cols].T.reshape(4, 2, 32, cols)
    block[1 - c] = total[cols:].T.reshape(4, 2, 32, cols)
    for dy in range(2):
        to = (1 - y0) if dy else y0
        for y1 in range(4):
            for j in range(2):
                lo = at + 32 * y1
                outs[dy][lo : lo + 32, cols * j : cols * j + cols] = block[j, y1, to]


def own_kernel(d_ref, s_ref, t_ref, *refs):
    outs, (block, mean) = refs[:2], refs[2:]
    cols = d_ref.shape[1]
    rows = d_ref.shape[0] - 8
    c = lax.axis_index("c")
    turn(d_ref[0:rows, :], t_ref, 0)
    turn(s_ref[0:rows, :], t_ref, cols)
    deal(against(t_ref, d_ref[0:rows, :]), block, outs, 0)
    mean[c] = d_ref[rows : rows + 8, :]
    mean[1 - c] = s_ref[rows : rows + 8, :]
    for out in outs:
        out[128:136, :] = jnp.zeros((8, 2 * cols), F32)
        for j in range(2):
            out[128:129, cols * j : cols * j + cols] = mean[j, 0:1, :]
        out[129:130, 0:cols] = d_ref[rows : rows + 1, :]


def near_kernel(t_ref, up_ref, down_ref, *refs):
    outs, block = refs[:2], refs[2]
    rows, cols = up_ref.shape[0] - 8, up_ref.shape[1]
    for k, ref in enumerate((up_ref, down_ref)):
        deal(against(t_ref, ref[0:rows, :]), block, outs, 128 * k)
    for out in outs:
        out[256:264, :] = jnp.zeros((8, 2 * cols), F32)
        for k, ref in enumerate((up_ref, down_ref)):
            out[256 + k : 257 + k, 0:cols] = ref[rows : rows + 1, :]


def far_kernel(up_ref, down_ref, cross_ref, *refs):
    outs, (block, mean) = refs[:4], refs[4:]
    rows, cols = up_ref.shape[0] - 8, up_ref.shape[1]
    z0, y0 = lax.axis_index("z0"), lax.axis_index("y0")
    crossed = jnp.full((1, cols), lax.axis_index("x") >= 2)
    other = jnp.where(crossed, cross_ref[...], down_ref[...])
    high, low = split(up_ref[0:rows, :].T)
    right_high, right_low = split(other[0:rows])
    product = jnp.dot(high, right_high, preferred_element_type=F32) + (
        jnp.dot(low, right_high, preferred_element_type=F32) + jnp.dot(high, right_low, preferred_element_type=F32)
    )
    block[0] = product.reshape(4, 2, 32, cols)
    block[1] = product.T.reshape(4, 2, 32, cols)
    mean[0] = up_ref[rows : rows + 8, :]
    mean[1] = other[rows : rows + 8]
    for p, out in enumerate(outs):
        dy, s = divmod(p, 2)
        kind = (1 - z0) if s else z0
        to = (1 - y0) if dy else y0
        for y1 in range(4):
            out[32 * y1 : 32 * y1 + 32, :] = block[kind, y1, to]
        out[128:129, :] = mean[kind, 0:1, :]
        out[129:130, :] = mean[1 - kind, 0:1, :]
        out[130:136, :] = jnp.zeros((6, cols), F32)


def merge_pair_kernel(*refs):
    groups = (refs[0:3], refs[3:6])
    keep_ref, send_ref, parts = refs[6:]
    cols = keep_ref.shape[1]
    z0, c = lax.axis_index("z0"), lax.axis_index("c")
    kept = jnp.full((1, 2 * cols), z0 == c)

    def read(group, lo, n):
        return jnp.where(kept, group[0][lo : lo + n, :], group[1][lo : lo + n, :]), group[2][lo : lo + n, :]

    def put(lo, value):
        n = value.shape[0]
        for j in range(2):
            parts[j, lo : lo + n, :] = value[:, cols * j : cols * j + cols]

    for group, n, at in zip(groups, (1, 2), (0, 128), strict=True):
        one, two = read(group, 0, 128 * n)
        put(at, one + two)
    own = read(groups[0], 128, 8)
    near = read(groups[1], 256, 8)
    for dy in range(2):
        put(384 + dy, own[dy][0:1, :])
        for k, m in enumerate((own[dy][1:2, :], near[dy][0:1, :], near[dy][1:2, :])):
            for j in range(2):
                parts[j, 386 + 2 * k + dy : 387 + 2 * k + dy, :] = m[:, 0:cols]
    keep_ref[...] = parts[c]
    send_ref[...] = parts[1 - c]


def merge_block_kernel(count, keep_ref, recv_ref, *refs):
    far, (out_ref, shift) = refs[:4], refs[4:]
    cols = keep_ref.shape[1]
    x, y0 = lax.axis_index("x"), lax.axis_index("y0")
    zeros = jnp.zeros((4, cols), F32)

    def mean_of(means):
        return jnp.sum(means, axis=0, keepdims=True) * 0.25

    def pairs(lo):
        return jnp.concatenate([keep_ref[lo : lo + 2, :], recv_ref[lo : lo + 2, :]], axis=0)

    own_means = pairs(384)
    own_mean = mean_of(own_means)
    for k, step in enumerate((0, 1, 3, 2)):
        if k < 3:
            means, right = pairs(386 + 2 * k), own_means
        else:
            means = jnp.concatenate([f[128:129, :] for f in far], axis=0)
            right = jnp.concatenate([f[129:130, :] for f in far], axis=0)
        mean = mean_of(means)
        left = jnp.concatenate([means - mean, zeros], axis=0)
        right = jnp.concatenate([right - own_mean, zeros], axis=0)
        shift[...] = (outer(left, right) * float(count)).reshape(4, 2, 32, cols)
        to = lax.rem(x + step, 4)
        for y1 in range(4):
            if k < 3:
                lo = 128 * k + 32 * y1
                total = keep_ref[lo : lo + 32, :] + recv_ref[lo : lo + 32, :]
            else:
                lo = 32 * y1
                total = (far[0][lo : lo + 32, :] + far[1][lo : lo + 32, :]) + (
                    far[2][lo : lo + 32, :] + far[3][lo : lo + 32, :]
                )
            out_ref[4 * to + y1, 0:32, :] = total + shift[y1, y0]
            out_ref[4 * to + y1, 32:33, :] = own_mean
            out_ref[4 * to + y1, 33:34, :] = mean
            out_ref[4 * to + y1, 34:40, :] = jnp.zeros((6, cols), F32)


def merge_all_kernel(count, in_ref, cov_ref, mean_ref, shift):
    blocks, _, cols = in_ref.shape
    total = in_ref[0, 0:32, :]
    for s in range(1, blocks):
        total = total + in_ref[s, 0:32, :]
    own = jnp.concatenate([in_ref[s, 32:33, :] for s in range(blocks)], axis=0)
    other = jnp.concatenate([in_ref[s, 33:34, :] for s in range(blocks)], axis=0)
    own_mean = jnp.sum(own, axis=0, keepdims=True) * (1.0 / blocks)
    other_mean = jnp.sum(other, axis=0, keepdims=True) * (1.0 / blocks)
    y = 2 * lax.axis_index("y1") + lax.axis_index("y0")
    shift[...] = (outer(other - other_mean, own - own_mean) * float(count)).reshape(8, 32, cols)
    cov_ref[...] = (total + shift[y]) / float(count * blocks - 1)
    mean_ref[...] = own_mean


def call(kernel, outs, args, scratch=(), mib=16, flops=0, moved=0):
    return pl.pallas_call(
        kernel,
        out_shape=outs,
        in_specs=[VMEM] * len(args),
        out_specs=jax.tree.map(lambda _: VMEM, outs),
        scratch_shapes=scratch,
        compiler_params=pltpu.CompilerParams(vmem_limit_bytes=mib * 2**20),
        cost_estimate=pl.CostEstimate(flops=flops, bytes_accessed=moved, transcendentals=0),
    )(*args)


def shifted(piece, axis, by):
    size = lax.axis_size(axis)
    return lax.ppermute(piece, axis, [(i, (i + by) % size) for i in range(size)])


def dealt(piece, dy):
    pairs = []
    for i in range(8):
        z0, y0, c = i // 4, i // 2 % 2, i % 2
        j = c * 4 + (y0 ^ dy) * 2 + z0
        if i != j:
            pairs.append((i, j))
    return lax.ppermute(piece, ("z0", "y0", "c"), pairs)


def between(piece, dy, s):
    pairs = []
    for i in range(32):
        z0, y0, x, c = i // 16, i // 8 % 2, i // 2 % 4, i % 2
        j = 1 - c if x >= 2 else c
        x_to, z_to, c_to = ((x + 1) % 4, j, c) if z0 ^ s else ((x + 3) % 4, c, j)
        pairs.append((i, z_to * 16 + (y0 ^ dy) * 8 + x_to * 2 + c_to))
    return lax.ppermute(piece, ("z0", "y0", "x", "c"), pairs)


def crossed(piece):
    return lax.ppermute(piece, ("x", "c"), [(4, 5), (5, 4), (6, 7), (7, 6)])


def steps(x):
    rows, cols = x.shape
    d = call(centre_kernel, shape(rows + 8, cols), (x,), flops=10**9, moved=2**21)
    up = shifted(d, "x", -1)
    down = shifted(d, "x", 1)
    swap = shifted(d, "c", 1)
    block = pltpu.VMEM((2, 4, 2, 32, cols), F32)
    mean = pltpu.VMEM((2, 8, cols), F32)
    t, *own = call(
        own_kernel,
        (shape(4 * cols, rows, dtype=BF16), *[shape(136, 2 * cols)] * 2),
        (d, swap),
        (block, mean),
        flops=2 * 10**9,
        moved=2**22,
    )
    near = call(near_kernel, [shape(264, 2 * cols)] * 2, (t, up, down), (block,), flops=4 * 10**9, moved=2**22)
    cross = crossed(down)
    far = call(far_kernel, [shape(136, cols)] * 4, (up, down, cross), (block, mean), flops=10**9, moved=2**22)
    far = [between(far[p], *divmod(p, 2)) for p in range(4)]
    sums = []
    for outs in (own, near):
        sums += [outs[0]] + [dealt(outs[dy], dy) for dy in range(2)]
    keep, send = call(
        merge_pair_kernel,
        [shape(392, cols)] * 2,
        sums,
        (pltpu.VMEM((2, 392, cols), F32),),
        flops=10**9,
        moved=2**22,
    )
    recv = shifted(send, "c", 1)
    merged = call(
        functools.partial(merge_block_kernel, rows),
        shape(16, 40, cols),
        (keep, recv, *far),
        (pltpu.VMEM((4, 2, 32, cols), F32),),
        flops=10**9,
        moved=2**22,
    )
    merged = lax.all_to_all(merged, ("z1", "y1"), 0, 0, tiled=True)
    covariance, mean = call(
        functools.partial(merge_all_kernel, 4 * rows),
        (shape(32, cols), shape(1, cols)),
        (merged,),
        (pltpu.VMEM((8, 32, cols), F32),),
        flops=10**9,
        moved=2**20,
    )
    return covariance, mean.reshape(cols)


def solution(mesh):
    finer = Mesh(mesh.devices.reshape(4, 2, 4, 2, 4, 2), SCEN + FAC)
    return jax.shard_map(
        steps,
        mesh=finer,
        in_specs=(P(SCEN, FAC),),
        out_specs=(P(SCEN, FAC), P(FAC)),
        check_vma=False,
    )
```

time: 115 us -> 125 us (1.087)
  the two profiles are of different devices: /device:TPU:64 before, /device:TPU:1 now
where the time goes in v1:
time: 125 us; the launch traced here: 124 us
  starting transfers between devices  46.5 us (37%)
  waiting for transfers between devices  35 us (28%)
  blocking collectives  33.8 us (27%)
  Pallas kernels  7.05 us (6%)
    all_to_all x1, blocking collectives, steps(): merged = lax.all_to_all(merged, ('z1', 'y1'), 0, 0, tiled=True)  33.8 us
    ppermute x4, waiting for transfers between devices, shifted(): lax.ppermute(piece, axis, [(i, (i + by) % size) for i in range(size)])  20.6 us
    ppermute x4, starting transfers between devices, shifted(): lax.ppermute(piece, axis, [(i, (i + by) % size) for i in range(size)])  17.9 us
    ppermute x4, starting transfers between devices, between(): return lax.ppermute(piece, ('z0', 'y0', 'x', 'c'), pairs)  15.9 us
    ppermute x4, starting transfers between devices, dealt(): return lax.ppermute(piece, ('z0', 'y0', 'c'), pairs)  12 us
    ppermute x4, waiting for transfers between devices, dealt(): return lax.ppermute(piece, ('z0', 'y0', 'c'), pairs)  10.7 us
    pallas_call x7, Pallas kernels, call(): pl.pallas_call(kernel, out_shape=outs, in_specs=[VMEM] * len(args), out_s...  7.05 us
    ppermute x4, waiting for transfers between devices, between(): return lax.ppermute(piece, ('z0', 'y0', 'x', 'c'), pairs)  3.64 us
  transfers between devices with their start and end apart: 13, of which 5 were waited for; matrix products, arithmetic and copies ran while one was open for 0% of the time, Pallas kernels for 4%

profile of v1, /device:TPU:1, one launch (start us, length us, event | category | flops | bytes accessed | tf_op | source)
XLA Modules:
  0.0 124.4 jit_solution(1717895268728438668)
XLA Ops:
  0.6 1.2 copy-done
  2.1 3.9 %collective-permute-start.4 = (f32[1032,256]{1,0:T(8,128)S(1)}, f32[1032,256]{1,0:T(8,128)S(1)}, u32[]{:S(2)}, u32[]{:S(2)}) collective-permute-start(f32[1032,256]{1,0:T(8,128)S(1)} %shard_map.30.d_ref), channel_id=1, source_target_pairs={{0,2},{2,4},{4,6},{6,0},{1,3},{3,5},{5,7},{7,1},{8,10},{10,12},{12... | collective-permute-start | bytes 3170312 | tf_op jit(solution)/shard_map/ppermute | solution.py:225
  6.0 6.7 %collective-permute-start = (f32[1032,256]{1,0:T(8,128)S(1)}, f32[1032,256]{1,0:T(8,128)S(1)}, u32[]{:S(2)}, u32[]{:S(2)}) collective-permute-start(f32[1032,256]{1,0:T(8,128)S(1)} %shard_map.30.d_ref), channel_id=1, source_target_pairs={{0,1},{1,0},{2,3},{3,2},{4,5},{5,4},{6,7},{7,6},{8,9},{9,8},{10,11... | collective-permute-start | bytes 3170312 | tf_op jit(solution)/shard_map/ppermute | solution.py:225
  12.8 4.9 %collective-permute-start.3 = (f32[1032,256]{1,0:T(8,128)S(1)}, f32[1032,256]{1,0:T(8,128)S(1)}, u32[]{:S(2)}, u32[]{:S(2)}) collective-permute-start(f32[1032,256]{1,0:T(8,128)S(1)} %shard_map.30.d_ref), channel_id=1, source_target_pairs={{0,6},{2,0},{4,2},{6,4},{1,7},{3,1},{5,3},{7,5},{8,14},{10,8},{12,... | collective-permute-start | bytes 3170312 | tf_op jit(solution)/shard_map/ppermute | solution.py:225
  17.6 6.9 %collective-permute-done.4.down_ref = f32[1032,256]{1,0:T(8,128)S(1)} collective-permute-done((f32[1032,256]{1,0:T(8,128)S(1)}, f32[1032,256]{1,0:T(8,128)S(1)}, u32[]{:S(2)}, u32[]{:S(2)}) %collective-permute-start.4) | collective-permute-done | bytes 1056800 | tf_op jit(solution)/shard_map/ppermute | solution.py:225
  25.2 1.3 %shard_map.31 = (bf16[1024,1024]{1,0:T(8,128)(2,1)S(1)}, f32[136,512]{1,0:T(8,128)S(1)}, f32[136,512]{1,0:T(8,128)S(1)}) custom-call(f32[1032,256]{1,0:T(8,128)S(1)} %shard_map.30.d_ref, f32[1032,256]{1,0:T(8,128)S(1)} %collective-permute-done.s_ref), custom_call_target="tpu_custom_call" | custom-call | flops 2000000000 | bytes 4194304 | tf_op jit(solution)/shard_map/pallas_call | solution.py:212
  26.5 13.8 %collective-permute-done.3.up_ref = f32[1032,256]{1,0:T(8,128)S(1)} collective-permute-done((f32[1032,256]{1,0:T(8,128)S(1)}, f32[1032,256]{1,0:T(8,128)S(1)}, u32[]{:S(2)}, u32[]{:S(2)}) %collective-permute-start.3) | collective-permute-done | bytes 1056800 | tf_op jit(solution)/shard_map/ppermute | solution.py:225
  40.3 2.2 %shard_map.32 = (f32[264,512]{1,0:T(8,128)S(1)}, f32[264,512]{1,0:T(8,128)S(1)}) custom-call(bf16[1024,1024]{1,0:T(8,128)(2,1)S(1)} %get-tuple-element.17.t_ref, f32[1032,256]{1,0:T(8,128)S(1)} %collective-permute-done.3.up_ref, f32[1032,256]{1,0:T(8,128)S(1)} %collective-permute-done.4.down_ref), custom_call_target="tpu_custom_call" | custom-call | flops 4000000000 | bytes 4194304 | tf_op jit(solution)/shard_map/pallas_call | solution.py:212
  42.5 1.9 %collective-permute-start.5 = (f32[264,512]{1,0:T(8,128)S(1)}, f32[264,512]{1,0:T(8,128)S(1)}, u32[]{:S(2)}, u32[]{:S(2)}) collective-permute-start(f32[264,512]{1,0:T(8,128)S(1)} %get-tuple-element.18.refs_3_), channel_id=1, source_target_pairs={{1,64},{9,72},{64,1},{72,9},{3,66},{11,74},{66,3},{74,11},{5,68},{... | collective-permute-start | bytes 1622024 | tf_op jit(solution)/shard_map/ppermute | solution.py:235
  44.4 1.9 %collective-permute-start.6 = (f32[264,512]{1,0:T(8,128)S(1)}, f32[264,512]{1,0:T(8,128)S(1)}, u32[]{:S(2)}, u32[]{:S(2)}) collective-permute-start(f32[264,512]{1,0:T(8,128)S(1)} %get-tuple-element.19), channel_id=1, source_target_pairs={{0,8},{1,72},{8,0},{9,64},{64,9},{65,73},{72,1},{73,65},{2,10},{3,... | collective-permute-start | bytes 1622024 | tf_op jit(solution)/shard_map/ppermute | solution.py:235
  46.3 3.6 %collective-permute-start.1 = (f32[136,512]{1,0:T(8,128)S(1)}, f32[136,512]{1,0:T(8,128)S(1)}, u32[]{:S(2)}, u32[]{:S(2)}) collective-permute-start(f32[136,512]{1,0:T(8,128)S(1)} %get-tuple-element.15.refs_0_), channel_id=1, source_target_pairs={{1,64},{9,72},{64,1},{72,9},{3,66},{11,74},{66,3},{74,11},{5,68},{... | collective-permute-start | bytes 835592 | tf_op jit(solution)/shard_map/ppermute | solution.py:235
  50.0 4.5 %collective-permute-start.2 = (f32[136,512]{1,0:T(8,128)S(1)}, f32[136,512]{1,0:T(8,128)S(1)}, u32[]{:S(2)}, u32[]{:S(2)}) collective-permute-start(f32[136,512]{1,0:T(8,128)S(1)} %get-tuple-element.16), channel_id=1, source_target_pairs={{0,8},{1,72},{8,0},{9,64},{64,9},{65,73},{72,1},{73,65},{2,10},{3,... | collective-permute-start | bytes 835592 | tf_op jit(solution)/shard_map/ppermute | solution.py:235
  54.5 10.7 %collective-permute-done.1.refs_1_ = f32[136,512]{1,0:T(8,128)S(1)} collective-permute-done((f32[136,512]{1,0:T(8,128)S(1)}, f32[136,512]{1,0:T(8,128)S(1)}, u32[]{:S(2)}, u32[]{:S(2)}) %collective-permute-start.1) | collective-permute-done | bytes 278560 | tf_op jit(solution)/shard_map/ppermute | solution.py:235
  65.5 2.4 %collective-permute-start.7 = (f32[392,256]{1,0:T(8,128)S(1)}, f32[392,256]{1,0:T(8,128)S(1)}, u32[]{:S(2)}, u32[]{:S(2)}) collective-permute-start(f32[392,256]{1,0:T(8,128)S(1)} %get-tuple-element.21), channel_id=1, source_target_pairs={{0,1},{1,0},{2,3},{3,2},{4,5},{5,4},{6,7},{7,6},{8,9},{9,8},{10,11... | collective-permute-start | bytes 1204232 | tf_op jit(solution)/shard_map/ppermute | solution.py:225
  67.9 0.9 shard_map.34
  68.8 2.7 %collective-permute-start.10 = (f32[136,256]{1,0:T(8,128)S(1)}, f32[136,256]{1,0:T(8,128)S(1)}, u32[]{:S(2)}, u32[]{:S(2)}) collective-permute-start(f32[136,256]{1,0:T(8,128)S(1)} %get-tuple-element.23), channel_id=1, source_target_pairs={{0,2},{1,67},{2,4},{3,69},{4,70},{5,7},{6,64},{7,1},{8,10},{9,75},... | collective-permute-start | bytes 417800 | tf_op jit(solution)/shard_map/ppermute | solution.py:245
  71.5 6.3 %collective-permute-start.11 = (f32[136,256]{1,0:T(8,128)S(1)}, f32[136,256]{1,0:T(8,128)S(1)}, u32[]{:S(2)}, u32[]{:S(2)}) collective-permute-start(f32[136,256]{1,0:T(8,128)S(1)} %get-tuple-element.24), channel_id=1, source_target_pairs={{0,14},{1,79},{2,8},{3,73},{4,11},{5,74},{6,13},{7,76},{8,6},{9,71... | collective-permute-start | bytes 417800 | tf_op jit(solution)/shard_map/ppermute | solution.py:245
  77.7 1.9 %collective-permute-start.12 = (f32[136,256]{1,0:T(8,128)S(1)}, f32[136,256]{1,0:T(8,128)S(1)}, u32[]{:S(2)}, u32[]{:S(2)}) collective-permute-start(f32[136,256]{1,0:T(8,128)S(1)} %get-tuple-element.25), channel_id=1, source_target_pairs={{0,10},{1,75},{2,12},{3,77},{4,78},{5,15},{6,72},{7,9},{8,2},{9,67... | collective-permute-start | bytes 417800 | tf_op jit(solution)/shard_map/ppermute | solution.py:245
  79.7 5.0 %collective-permute-start.9 = (f32[136,256]{1,0:T(8,128)S(1)}, f32[136,256]{1,0:T(8,128)S(1)}, u32[]{:S(2)}, u32[]{:S(2)}) collective-permute-start(f32[136,256]{1,0:T(8,128)S(1)} %get-tuple-element.22), channel_id=1, source_target_pairs={{0,6},{1,71},{2,0},{3,65},{4,3},{5,66},{6,5},{7,68},{8,14},{9,79},... | collective-permute-start | bytes 417800 | tf_op jit(solution)/shard_map/ppermute | solution.py:245
  84.7 2.6 %collective-permute-done.12.refs_3_ = f32[136,256]{1,0:T(8,128)S(1)} collective-permute-done((f32[136,256]{1,0:T(8,128)S(1)}, f32[136,256]{1,0:T(8,128)S(1)}, u32[]{:S(2)}, u32[]{:S(2)}) %collective-permute-start.12) | collective-permute-done | bytes 139296 | tf_op jit(solution)/shard_map/ppermute | solution.py:245
  87.3 1.0 collective-permute-done.9.refs_0_
  88.3 1.2 shard_map.35
  89.5 33.8 %all_to_all.5.in_ref = f32[16,40,256]{2,1,0:T(8,128)S(1)} all-to-all(f32[16,40,256]{2,1,0:T(8,128)S(1)} %shard_map.35), channel_id=1, replica_groups=mesh['z1'=4,'z0'=2,'y1'=4,'y0'=2,'x'=4,'c'=2] {'z1','y1'}, dimensions={0} | all-to-all | bytes 1310720 | tf_op jit(solution)/shard_map/all_to_all | solution.py:292
  123.3 1.1 shard_map.36
  (12 shorter events, 1.2 us)
Async XLA Ops:
  0.6 1.2 copy-start
  2.1 22.4 %collective-permute-start.4 = (f32[1032,256]{1,0:T(8,128)S(1)}, f32[1032,256]{1,0:T(8,128)S(1)}, u32[]{:S(2)}, u32[]{:S(2)}) collective-permute-start(f32[1032,256]{1,0:T(8,128)S(1)} %shard_map.30.d_ref), channel_id=1, source_target_pairs={{0,2},{2,4},{4,6},{6,0},{1,3},{3,5},{5,7},{7,1},{8,10},{10,12},{12... | collective-permute-start | bytes 3170312 | tf_op jit(solution)/shard_map/ppermute | solution.py:225
  6.0 19.2 %collective-permute-start = (f32[1032,256]{1,0:T(8,128)S(1)}, f32[1032,256]{1,0:T(8,128)S(1)}, u32[]{:S(2)}, u32[]{:S(2)}) collective-permute-start(f32[1032,256]{1,0:T(8,128)S(1)} %shard_map.30.d_ref), channel_id=1, source_target_pairs={{0,1},{1,0},{2,3},{3,2},{4,5},{5,4},{6,7},{7,6},{8,9},{9,8},{10,11... | collective-permute-start | bytes 3170312 | tf_op jit(solution)/shard_map/ppermute | solution.py:225
  12.8 27.5 %collective-permute-start.3 = (f32[1032,256]{1,0:T(8,128)S(1)}, f32[1032,256]{1,0:T(8,128)S(1)}, u32[]{:S(2)}, u32[]{:S(2)}) collective-permute-start(f32[1032,256]{1,0:T(8,128)S(1)} %shard_map.30.d_ref), channel_id=1, source_target_pairs={{0,6},{2,0},{4,2},{6,4},{1,7},{3,1},{5,3},{7,5},{8,14},{10,8},{12,... | collective-permute-start | bytes 3170312 | tf_op jit(solution)/shard_map/ppermute | solution.py:225
  24.5 43.4 %collective-permute-start.8 = (f32[1032,256]{1,0:T(8,128)S(1)}, f32[1032,256]{1,0:T(8,128)S(1)}, u32[]{:S(2)}, u32[]{:S(2)}) collective-permute-start(f32[1032,256]{1,0:T(8,128)S(1)} %collective-permute-done.4.down_ref), channel_id=1, source_target_pairs={{4,5},{5,4},{6,7},{7,6},{12,13},{13,12},{14,15},{15,14},{20,21},{2... | collective-permute-start | bytes 3170312 | tf_op jit(solution)/shard_map/ppermute | solution.py:249
  42.5 22.7 %collective-permute-start.5 = (f32[264,512]{1,0:T(8,128)S(1)}, f32[264,512]{1,0:T(8,128)S(1)}, u32[]{:S(2)}, u32[]{:S(2)}) collective-permute-start(f32[264,512]{1,0:T(8,128)S(1)} %get-tuple-element.18.refs_3_), channel_id=1, source_target_pairs={{1,64},{9,72},{64,1},{72,9},{3,66},{11,74},{66,3},{74,11},{5,68},{... | collective-permute-start | bytes 1622024 | tf_op jit(solution)/shard_map/ppermute | solution.py:235
  44.4 20.8 %collective-permute-start.6 = (f32[264,512]{1,0:T(8,128)S(1)}, f32[264,512]{1,0:T(8,128)S(1)}, u32[]{:S(2)}, u32[]{:S(2)}) collective-permute-start(f32[264,512]{1,0:T(8,128)S(1)} %get-tuple-element.19), channel_id=1, source_target_pairs={{0,8},{1,72},{8,0},{9,64},{64,9},{65,73},{72,1},{73,65},{2,10},{3,... | collective-permute-start | bytes 1622024 | tf_op jit(solution)/shard_map/ppermute | solution.py:235
  46.3 18.9 %collective-permute-start.1 = (f32[136,512]{1,0:T(8,128)S(1)}, f32[136,512]{1,0:T(8,128)S(1)}, u32[]{:S(2)}, u32[]{:S(2)}) collective-permute-start(f32[136,512]{1,0:T(8,128)S(1)} %get-tuple-element.15.refs_0_), channel_id=1, source_target_pairs={{1,64},{9,72},{64,1},{72,9},{3,66},{11,74},{66,3},{74,11},{5,68},{... | collective-permute-start | bytes 835592 | tf_op jit(solution)/shard_map/ppermute | solution.py:235
  50.0 15.2 %collective-permute-start.2 = (f32[136,512]{1,0:T(8,128)S(1)}, f32[136,512]{1,0:T(8,128)S(1)}, u32[]{:S(2)}, u32[]{:S(2)}) collective-permute-start(f32[136,512]{1,0:T(8,128)S(1)} %get-tuple-element.16), channel_id=1, source_target_pairs={{0,8},{1,72},{8,0},{9,64},{64,9},{65,73},{72,1},{73,65},{2,10},{3,... | collective-permute-start | bytes 835592 | tf_op jit(solution)/shard_map/ppermute | solution.py:235
  65.5 19.2 %collective-permute-start.7 = (f32[392,256]{1,0:T(8,128)S(1)}, f32[392,256]{1,0:T(8,128)S(1)}, u32[]{:S(2)}, u32[]{:S(2)}) collective-permute-start(f32[392,256]{1,0:T(8,128)S(1)} %get-tuple-element.21), channel_id=1, source_target_pairs={{0,1},{1,0},{2,3},{3,2},{4,5},{5,4},{6,7},{7,6},{8,9},{9,8},{10,11... | collective-permute-start | bytes 1204232 | tf_op jit(solution)/shard_map/ppermute | solution.py:225
  68.8 15.9 %collective-permute-start.10 = (f32[136,256]{1,0:T(8,128)S(1)}, f32[136,256]{1,0:T(8,128)S(1)}, u32[]{:S(2)}, u32[]{:S(2)}) collective-permute-start(f32[136,256]{1,0:T(8,128)S(1)} %get-tuple-element.23), channel_id=1, source_target_pairs={{0,2},{1,67},{2,4},{3,69},{4,70},{5,7},{6,64},{7,1},{8,10},{9,75},... | collective-permute-start | bytes 417800 | tf_op jit(solution)/shard_map/ppermute | solution.py:245
  71.5 13.2 %collective-permute-start.11 = (f32[136,256]{1,0:T(8,128)S(1)}, f32[136,256]{1,0:T(8,128)S(1)}, u32[]{:S(2)}, u32[]{:S(2)}) collective-permute-start(f32[136,256]{1,0:T(8,128)S(1)} %get-tuple-element.24), channel_id=1, source_target_pairs={{0,14},{1,79},{2,8},{3,73},{4,11},{5,74},{6,13},{7,76},{8,6},{9,71... | collective-permute-start | bytes 417800 | tf_op jit(solution)/shard_map/ppermute | solution.py:245
  77.7 9.5 %collective-permute-start.12 = (f32[136,256]{1,0:T(8,128)S(1)}, f32[136,256]{1,0:T(8,128)S(1)}, u32[]{:S(2)}, u32[]{:S(2)}) collective-permute-start(f32[136,256]{1,0:T(8,128)S(1)} %get-tuple-element.25), channel_id=1, source_target_pairs={{0,10},{1,75},{2,12},{3,77},{4,78},{5,15},{6,72},{7,9},{8,2},{9,67... | collective-permute-start | bytes 417800 | tf_op jit(solution)/shard_map/ppermute | solution.py:245
  79.7 8.7 %collective-permute-start.9 = (f32[136,256]{1,0:T(8,128)S(1)}, f32[136,256]{1,0:T(8,128)S(1)}, u32[]{:S(2)}, u32[]{:S(2)}) collective-permute-start(f32[136,256]{1,0:T(8,128)S(1)} %get-tuple-element.22), channel_id=1, source_target_pairs={{0,6},{1,71},{2,0},{3,65},{4,3},{5,66},{6,5},{7,68},{8,14},{9,79},... | collective-permute-start | bytes 417800 | tf_op jit(solution)/shard_map/ppermute | solution.py:245

commit v2 on v1

--- a/solution.py
+++ b/solution.py
@@ -87,12 +87,18 @@
         out[129:130, 0:cols] = d_ref[rows : rows + 1, :]
 
 
+def above_kernel(t_ref, up_ref, *refs):
+    outs, block = refs[:2], refs[2]
+    rows = up_ref.shape[0] - 8
+    deal(against(t_ref, up_ref[0:rows, :]), block, outs, 0)
+
+
 def near_kernel(t_ref, up_ref, down_ref, *refs):
-    outs, block = refs[:2], refs[2]
+    above, outs, block = refs[:2], refs[2:4], refs[4]
     rows, cols = up_ref.shape[0] - 8, up_ref.shape[1]
-    for k, ref in enumerate((up_ref, down_ref)):
-        deal(against(t_ref, ref[0:rows, :]), block, outs, 128 * k)
-    for out in outs:
+    deal(against(t_ref, down_ref[0:rows, :]), block, outs, 128)
+    for part, out in zip(above, outs, strict=True):
+        out[0:128, :] = part[...]
         out[256:264, :] = jnp.zeros((8, 2 * cols), F32)
         for k, ref in enumerate((up_ref, down_ref)):
             out[256 + k : 257 + k, 0:cols] = ref[rows : rows + 1, :]
@@ -103,16 +109,16 @@
     rows, cols = up_ref.shape[0] - 8, up_ref.shape[1]
     z0, y0 = lax.axis_index("z0"), lax.axis_index("y0")
     crossed = jnp.full((1, cols), lax.axis_index("x") >= 2)
-    other = jnp.where(crossed, cross_ref[...], down_ref[...])
-    high, low = split(up_ref[0:rows, :].T)
-    right_high, right_low = split(other[0:rows])
+    above = jnp.where(crossed, cross_ref[...], up_ref[...])
+    high, low = split(above[0:rows].T)
+    right_high, right_low = split(down_ref[0:rows, :])
     product = jnp.dot(high, right_high, preferred_element_type=F32) + (
         jnp.dot(low, right_high, preferred_element_type=F32) + jnp.dot(high, right_low, preferred_element_type=F32)
     )
     block[0] = product.reshape(4, 2, 32, cols)
     block[1] = product.T.reshape(4, 2, 32, cols)
-    mean[0] = up_ref[rows : rows + 8, :]
-    mean[1] = other[rows : rows + 8]
+    mean[0] = above[rows : rows + 8]
+    mean[1] = down_ref[rows : rows + 8, :]
     for p, out in enumerate(outs):
         dy, s = divmod(p, 2)
         kind = (1 - z0) if s else z0
@@ -167,16 +173,17 @@
 
     own_means = pairs(384)
     own_mean = mean_of(own_means)
+    far_means = jnp.concatenate([f[129:130, :] for f in far], axis=0)
+    right = jnp.concatenate([own_means - own_mean, far_means - own_mean], axis=0)
+    row_means, left = [], []
+    for k in range(4):
+        means = pairs(386 + 2 * k) if k < 3 else jnp.concatenate([f[128:129, :] for f in far], axis=0)
+        mean = mean_of(means)
+        row_means.append(mean)
+        left.append(jnp.concatenate([means - mean, zeros] if k < 3 else [zeros, means - mean], axis=0))
+    moved = outer(jnp.concatenate(left, axis=1), right) * float(count)
+    shift[...] = moved.reshape(4, 4, 2, 32, cols)
     for k, step in enumerate((0, 1, 3, 2)):
-        if k < 3:
-            means, right = pairs(386 + 2 * k), own_means
-        else:
-            means = jnp.concatenate([f[128:129, :] for f in far], axis=0)
-            right = jnp.concatenate([f[129:130, :] for f in far], axis=0)
-        mean = mean_of(means)
-        left = jnp.concatenate([means - mean, zeros], axis=0)
-        right = jnp.concatenate([right - own_mean, zeros], axis=0)
-        shift[...] = (outer(left, right) * float(count)).reshape(4, 2, 32, cols)
         to = lax.rem(x + step, 4)
         for y1 in range(4):
             if k < 3:
@@ -187,9 +194,9 @@
                 total = (far[0][lo : lo + 32, :] + far[1][lo : lo + 32, :]) + (
                     far[2][lo : lo + 32, :] + far[3][lo : lo + 32, :]
                 )
-            out_ref[4 * to + y1, 0:32, :] = total + shift[y1, y0]
+            out_ref[4 * to + y1, 0:32, :] = total + shift[k, y1, y0]
             out_ref[4 * to + y1, 32:33, :] = own_mean
-            out_ref[4 * to + y1, 33:34, :] = mean
+            out_ref[4 * to + y1, 33:34, :] = row_means[k]
             out_ref[4 * to + y1, 34:40, :] = jnp.zeros((6, cols), F32)
 
 
@@ -239,8 +246,8 @@
     pairs = []
     for i in range(32):
         z0, y0, x, c = i // 16, i // 8 % 2, i // 2 % 4, i % 2
-        j = 1 - c if x >= 2 else c
-        x_to, z_to, c_to = ((x + 1) % 4, j, c) if z0 ^ s else ((x + 3) % 4, c, j)
+        above = 1 - c if x >= 2 else c
+        x_to, z_to, c_to = ((x + 1) % 4, c, above) if z0 ^ s else ((x + 3) % 4, above, c)
         pairs.append((i, z_to * 16 + (y0 ^ dy) * 8 + x_to * 2 + c_to))
     return lax.ppermute(piece, ("z0", "y0", "x", "c"), pairs)
 
@@ -265,8 +272,9 @@
         flops=2 * 10**9,
         moved=2**22,
     )
-    near = call(near_kernel, [shape(264, 2 * cols)] * 2, (t, up, down), (block,), flops=4 * 10**9, moved=2**22)
-    cross = crossed(down)
+    cross = crossed(up)
+    above = call(above_kernel, [shape(128, 2 * cols)] * 2, (t, up), (block,), flops=2 * 10**9, moved=2**22)
+    near = call(near_kernel, [shape(264, 2 * cols)] * 2, (t, up, down, *above), (block,), flops=2 * 10**9, moved=2**22)
     far = call(far_kernel, [shape(136, cols)] * 4, (up, down, cross), (block, mean), flops=10**9, moved=2**22)
     far = [between(far[p], *divmod(p, 2)) for p in range(4)]
     sums = []
@@ -285,7 +293,7 @@
         functools.partial(merge_block_kernel, rows),
         shape(16, 40, cols),
         (keep, recv, *far),
-        (pltpu.VMEM((4, 2, 32, cols), F32),),
+        (pltpu.VMEM((4, 4, 2, 32, cols), F32),),
         flops=10**9,
         moved=2**22,
     )

time: 125 us -> 125 us (level)
  starting transfers between devices: 46.5 us -> 43.7 us
  blocking collectives: 33.8 us -> 35.4 us
  waiting for transfers between devices: 35 us -> 36.6 us
    all_to_all x1, blocking collectives: 33.8 us -> 35.4 us  [steps(): merged = lax.all_to_all(merged, ('z1', 'y1'), 0, 0, tiled=True)]
    ppermute x4, starting transfers between devices: 15.9 us -> 14.3 us  [between(): return lax.ppermute(piece, ('z0', 'y0', 'x', 'c'), pairs)]
    pallas_call x7 -> x8, Pallas kernels: 7.05 us -> 6.99 us  [call(): pl.pallas_call(kernel, out_shape=outs, in_specs=[VMEM] * len(args), out_s...]
  transfers between devices with their start and end apart: 13 -> 13, of which waited for: 5 -> 6; matrix products, arithmetic and copies ran while one was open for 0% -> 0% of each run, Pallas kernels for 4% -> 4%
where the time goes in v2:
time: 125 us
  starting transfers between devices  43.7 us (35%)
  waiting for transfers between devices  36.6 us (29%)
  blocking collectives  35.4 us (28%)
  Pallas kernels  6.99 us (6%)
    all_to_all x1, blocking collectives, steps(): merged = lax.all_to_all(merged, ('z1', 'y1'), 0, 0, tiled=True)  35.4 us
    ppermute x4, waiting for transfers between devices, shifted(): lax.ppermute(piece, axis, [(i, (i + by) % size) for i in range(size)])  21.2 us
    ppermute x4, starting transfers between devices, shifted(): lax.ppermute(piece, axis, [(i, (i + by) % size) for i in range(size)])  16.7 us
    ppermute x4, starting transfers between devices, between(): return lax.ppermute(piece, ('z0', 'y0', 'x', 'c'), pairs)  14.3 us
    ppermute x4, starting transfers between devices, dealt(): return lax.ppermute(piece, ('z0', 'y0', 'c'), pairs)  12 us
    ppermute x4, waiting for transfers between devices, dealt(): return lax.ppermute(piece, ('z0', 'y0', 'c'), pairs)  10.7 us
    pallas_call x8, Pallas kernels, call(): pl.pallas_call(kernel, out_shape=outs, in_specs=[VMEM] * len(args), out_s...  6.99 us
    ppermute x4, waiting for transfers between devices, between(): return lax.ppermute(piece, ('z0', 'y0', 'x', 'c'), pairs)  4.7 us
  transfers between devices with their start and end apart: 13, of which 6 were waited for; matrix products, arithmetic and copies ran while one was open for 0% of the time, Pallas kernels for 4%

profile of v2, /device:TPU:1, one launch (start us, length us, event | category | flops | bytes accessed | tf_op | source)
XLA Modules:
  0.0 124.8 jit_solution(10976107161647820516)
XLA Ops:
  0.6 1.2 copy-done
  2.1 5.2 %collective-permute-start.3 = (f32[1032,256]{1,0:T(8,128)S(1)}, f32[1032,256]{1,0:T(8,128)S(1)}, u32[]{:S(2)}, u32[]{:S(2)}) collective-permute-start(f32[1032,256]{1,0:T(8,128)S(1)} %shard_map.30.d_ref), channel_id=1, source_target_pairs={{0,6},{2,0},{4,2},{6,4},{1,7},{3,1},{5,3},{7,5},{8,14},{10,8},{12,... | collective-permute-start | bytes 3170312 | tf_op jit(solution)/shard_map/ppermute | solution.py:232
  7.3 5.5 %collective-permute-start = (f32[1032,256]{1,0:T(8,128)S(1)}, f32[1032,256]{1,0:T(8,128)S(1)}, u32[]{:S(2)}, u32[]{:S(2)}) collective-permute-start(f32[1032,256]{1,0:T(8,128)S(1)} %shard_map.30.d_ref), channel_id=1, source_target_pairs={{0,1},{1,0},{2,3},{3,2},{4,5},{5,4},{6,7},{7,6},{8,9},{9,8},{10,11... | collective-permute-start | bytes 3170312 | tf_op jit(solution)/shard_map/ppermute | solution.py:232
  12.8 3.6 %collective-permute-start.4 = (f32[1032,256]{1,0:T(8,128)S(1)}, f32[1032,256]{1,0:T(8,128)S(1)}, u32[]{:S(2)}, u32[]{:S(2)}) collective-permute-start(f32[1032,256]{1,0:T(8,128)S(1)} %shard_map.30.d_ref), channel_id=1, source_target_pairs={{0,2},{2,4},{4,6},{6,0},{1,3},{3,5},{5,7},{7,1},{8,10},{10,12},{12... | collective-permute-start | bytes 3170312 | tf_op jit(solution)/shard_map/ppermute | solution.py:232
  16.4 10.3 %collective-permute-done.3.up_ref = f32[1032,256]{1,0:T(8,128)S(1)} collective-permute-done((f32[1032,256]{1,0:T(8,128)S(1)}, f32[1032,256]{1,0:T(8,128)S(1)}, u32[]{:S(2)}, u32[]{:S(2)}) %collective-permute-start.3) | collective-permute-done | bytes 1056800 | tf_op jit(solution)/shard_map/ppermute | solution.py:232
  27.4 1.3 %shard_map.31 = (bf16[1024,1024]{1,0:T(8,128)(2,1)S(1)}, f32[136,512]{1,0:T(8,128)S(1)}, f32[136,512]{1,0:T(8,128)S(1)}) custom-call(f32[1032,256]{1,0:T(8,128)S(1)} %shard_map.30.d_ref, f32[1032,256]{1,0:T(8,128)S(1)} %collective-permute-done.s_ref), custom_call_target="tpu_custom_call" | custom-call | flops 2000000000 | bytes 4194304 | tf_op jit(solution)/shard_map/pallas_call | solution.py:219
  28.7 1.1 shard_map.32
  29.8 10.9 %collective-permute-done.4.down_ref = f32[1032,256]{1,0:T(8,128)S(1)} collective-permute-done((f32[1032,256]{1,0:T(8,128)S(1)}, f32[1032,256]{1,0:T(8,128)S(1)}, u32[]{:S(2)}, u32[]{:S(2)}) %collective-permute-start.4) | collective-permute-done | bytes 1056800 | tf_op jit(solution)/shard_map/ppermute | solution.py:232
  40.7 1.1 shard_map.33
  41.9 2.2 %collective-permute-start.5 = (f32[264,512]{1,0:T(8,128)S(1)}, f32[264,512]{1,0:T(8,128)S(1)}, u32[]{:S(2)}, u32[]{:S(2)}) collective-permute-start(f32[264,512]{1,0:T(8,128)S(1)} %get-tuple-element.22.refs_3_), channel_id=1, source_target_pairs={{1,64},{9,72},{64,1},{72,9},{3,66},{11,74},{66,3},{74,11},{5,68},{... | collective-permute-start | bytes 1622024 | tf_op jit(solution)/shard_map/ppermute | solution.py:242
  44.0 2.9 %collective-permute-start.6 = (f32[264,512]{1,0:T(8,128)S(1)}, f32[264,512]{1,0:T(8,128)S(1)}, u32[]{:S(2)}, u32[]{:S(2)}) collective-permute-start(f32[264,512]{1,0:T(8,128)S(1)} %get-tuple-element.23), channel_id=1, source_target_pairs={{0,8},{1,72},{8,0},{9,64},{64,9},{65,73},{72,1},{73,65},{2,10},{3,... | collective-permute-start | bytes 1622024 | tf_op jit(solution)/shard_map/ppermute | solution.py:242
  47.0 3.6 %collective-permute-start.1 = (f32[136,512]{1,0:T(8,128)S(1)}, f32[136,512]{1,0:T(8,128)S(1)}, u32[]{:S(2)}, u32[]{:S(2)}) collective-permute-start(f32[136,512]{1,0:T(8,128)S(1)} %get-tuple-element.17.refs_0_), channel_id=1, source_target_pairs={{1,64},{9,72},{64,1},{72,9},{3,66},{11,74},{66,3},{74,11},{5,68},{... | collective-permute-start | bytes 835592 | tf_op jit(solution)/shard_map/ppermute | solution.py:242
  50.6 3.3 %collective-permute-start.2 = (f32[136,512]{1,0:T(8,128)S(1)}, f32[136,512]{1,0:T(8,128)S(1)}, u32[]{:S(2)}, u32[]{:S(2)}) collective-permute-start(f32[136,512]{1,0:T(8,128)S(1)} %get-tuple-element.18), channel_id=1, source_target_pairs={{0,8},{1,72},{8,0},{9,64},{64,9},{65,73},{72,1},{73,65},{2,10},{3,... | collective-permute-start | bytes 835592 | tf_op jit(solution)/shard_map/ppermute | solution.py:242
  53.9 10.7 %collective-permute-done.1.refs_1_ = f32[136,512]{1,0:T(8,128)S(1)} collective-permute-done((f32[136,512]{1,0:T(8,128)S(1)}, f32[136,512]{1,0:T(8,128)S(1)}, u32[]{:S(2)}, u32[]{:S(2)}) %collective-permute-start.1) | collective-permute-done | bytes 278560 | tf_op jit(solution)/shard_map/ppermute | solution.py:242
  64.9 2.4 %collective-permute-start.7 = (f32[392,256]{1,0:T(8,128)S(1)}, f32[392,256]{1,0:T(8,128)S(1)}, u32[]{:S(2)}, u32[]{:S(2)}) collective-permute-start(f32[392,256]{1,0:T(8,128)S(1)} %get-tuple-element.25), channel_id=1, source_target_pairs={{0,1},{1,0},{2,3},{3,2},{4,5},{5,4},{6,7},{7,6},{8,9},{9,8},{10,11... | collective-permute-start | bytes 1204232 | tf_op jit(solution)/shard_map/ppermute | solution.py:232
  68.2 4.7 %collective-permute-start.10 = (f32[136,256]{1,0:T(8,128)S(1)}, f32[136,256]{1,0:T(8,128)S(1)}, u32[]{:S(2)}, u32[]{:S(2)}) collective-permute-start(f32[136,256]{1,0:T(8,128)S(1)} %get-tuple-element.27), channel_id=1, source_target_pairs={{0,2},{1,67},{2,4},{3,69},{4,7},{5,70},{6,1},{7,64},{8,10},{9,75},... | collective-permute-start | bytes 417800 | tf_op jit(solution)/shard_map/ppermute | solution.py:252
  72.9 1.9 %collective-permute-start.11 = (f32[136,256]{1,0:T(8,128)S(1)}, f32[136,256]{1,0:T(8,128)S(1)}, u32[]{:S(2)}, u32[]{:S(2)}) collective-permute-start(f32[136,256]{1,0:T(8,128)S(1)} %get-tuple-element.28), channel_id=1, source_target_pairs={{0,14},{1,79},{2,8},{3,73},{4,74},{5,11},{6,76},{7,13},{8,6},{9,71... | collective-permute-start | bytes 417800 | tf_op jit(solution)/shard_map/ppermute | solution.py:252
  74.8 2.9 %collective-permute-start.12 = (f32[136,256]{1,0:T(8,128)S(1)}, f32[136,256]{1,0:T(8,128)S(1)}, u32[]{:S(2)}, u32[]{:S(2)}) collective-permute-start(f32[136,256]{1,0:T(8,128)S(1)} %get-tuple-element.29), channel_id=1, source_target_pairs={{0,10},{1,75},{2,12},{3,77},{4,15},{5,78},{6,9},{7,72},{8,2},{9,67... | collective-permute-start | bytes 417800 | tf_op jit(solution)/shard_map/ppermute | solution.py:252
  77.7 4.8 %collective-permute-start.9 = (f32[136,256]{1,0:T(8,128)S(1)}, f32[136,256]{1,0:T(8,128)S(1)}, u32[]{:S(2)}, u32[]{:S(2)}) collective-permute-start(f32[136,256]{1,0:T(8,128)S(1)} %get-tuple-element.26), channel_id=1, source_target_pairs={{0,6},{1,71},{2,0},{3,65},{4,66},{5,3},{6,68},{7,5},{8,14},{9,79},... | collective-permute-start | bytes 417800 | tf_op jit(solution)/shard_map/ppermute | solution.py:252
  82.5 1.3 %collective-permute-done.11.refs_2_ = f32[136,256]{1,0:T(8,128)S(1)} collective-permute-done((f32[136,256]{1,0:T(8,128)S(1)}, f32[136,256]{1,0:T(8,128)S(1)}, u32[]{:S(2)}, u32[]{:S(2)}) %collective-permute-start.11) | collective-permute-done | bytes 139296 | tf_op jit(solution)/shard_map/ppermute | solution.py:252
  84.2 3.1 %collective-permute-done.9.refs_0_ = f32[136,256]{1,0:T(8,128)S(1)} collective-permute-done((f32[136,256]{1,0:T(8,128)S(1)}, f32[136,256]{1,0:T(8,128)S(1)}, u32[]{:S(2)}, u32[]{:S(2)}) %collective-permute-start.9) | collective-permute-done | bytes 139296 | tf_op jit(solution)/shard_map/ppermute | solution.py:252
  87.2 1.1 shard_map.36
  88.3 35.4 %all_to_all.5.in_ref = f32[16,40,256]{2,1,0:T(8,128)S(1)} all-to-all(f32[16,40,256]{2,1,0:T(8,128)S(1)} %shard_map.36), channel_id=1, replica_groups=mesh['z1'=4,'z0'=2,'y1'=4,'y0'=2,'x'=4,'c'=2] {'z1','y1'}, dimensions={0} | all-to-all | bytes 1310720 | tf_op jit(solution)/shard_map/all_to_all | solution.py:300
  123.8 1.1 shard_map.37
  (13 shorter events, 2.5 us)
Async XLA Ops:
  0.6 1.2 copy-start
  2.1 24.6 %collective-permute-start.3 = (f32[1032,256]{1,0:T(8,128)S(1)}, f32[1032,256]{1,0:T(8,128)S(1)}, u32[]{:S(2)}, u32[]{:S(2)}) collective-permute-start(f32[1032,256]{1,0:T(8,128)S(1)} %shard_map.30.d_ref), channel_id=1, source_target_pairs={{0,6},{2,0},{4,2},{6,4},{1,7},{3,1},{5,3},{7,5},{8,14},{10,8},{12,... | collective-permute-start | bytes 3170312 | tf_op jit(solution)/shard_map/ppermute | solution.py:232
  7.3 20.1 %collective-permute-start = (f32[1032,256]{1,0:T(8,128)S(1)}, f32[1032,256]{1,0:T(8,128)S(1)}, u32[]{:S(2)}, u32[]{:S(2)}) collective-permute-start(f32[1032,256]{1,0:T(8,128)S(1)} %shard_map.30.d_ref), channel_id=1, source_target_pairs={{0,1},{1,0},{2,3},{3,2},{4,5},{5,4},{6,7},{7,6},{8,9},{9,8},{10,11... | collective-permute-start | bytes 3170312 | tf_op jit(solution)/shard_map/ppermute | solution.py:232
  12.8 28.0 %collective-permute-start.4 = (f32[1032,256]{1,0:T(8,128)S(1)}, f32[1032,256]{1,0:T(8,128)S(1)}, u32[]{:S(2)}, u32[]{:S(2)}) collective-permute-start(f32[1032,256]{1,0:T(8,128)S(1)} %shard_map.30.d_ref), channel_id=1, source_target_pairs={{0,2},{2,4},{4,6},{6,0},{1,3},{3,5},{5,7},{7,1},{8,10},{10,12},{12... | collective-permute-start | bytes 3170312 | tf_op jit(solution)/shard_map/ppermute | solution.py:232
  26.7 40.6 %collective-permute-start.8 = (f32[1032,256]{1,0:T(8,128)S(1)}, f32[1032,256]{1,0:T(8,128)S(1)}, u32[]{:S(2)}, u32[]{:S(2)}) collective-permute-start(f32[1032,256]{1,0:T(8,128)S(1)} %collective-permute-done.3.up_ref), channel_id=1, source_target_pairs={{4,5},{5,4},{6,7},{7,6},{12,13},{13,12},{14,15},{15,14},{20,21},{2... | collective-permute-start | bytes 3170312 | tf_op jit(solution)/shard_map/ppermute | solution.py:256
  41.9 22.7 %collective-permute-start.5 = (f32[264,512]{1,0:T(8,128)S(1)}, f32[264,512]{1,0:T(8,128)S(1)}, u32[]{:S(2)}, u32[]{:S(2)}) collective-permute-start(f32[264,512]{1,0:T(8,128)S(1)} %get-tuple-element.22.refs_3_), channel_id=1, source_target_pairs={{1,64},{9,72},{64,1},{72,9},{3,66},{11,74},{66,3},{74,11},{5,68},{... | collective-permute-start | bytes 1622024 | tf_op jit(solution)/shard_map/ppermute | solution.py:242
  44.0 20.6 %collective-permute-start.6 = (f32[264,512]{1,0:T(8,128)S(1)}, f32[264,512]{1,0:T(8,128)S(1)}, u32[]{:S(2)}, u32[]{:S(2)}) collective-permute-start(f32[264,512]{1,0:T(8,128)S(1)} %get-tuple-element.23), channel_id=1, source_target_pairs={{0,8},{1,72},{8,0},{9,64},{64,9},{65,73},{72,1},{73,65},{2,10},{3,... | collective-permute-start | bytes 1622024 | tf_op jit(solution)/shard_map/ppermute | solution.py:242
  47.0 17.6 %collective-permute-start.1 = (f32[136,512]{1,0:T(8,128)S(1)}, f32[136,512]{1,0:T(8,128)S(1)}, u32[]{:S(2)}, u32[]{:S(2)}) collective-permute-start(f32[136,512]{1,0:T(8,128)S(1)} %get-tuple-element.17.refs_0_), channel_id=1, source_target_pairs={{1,64},{9,72},{64,1},{72,9},{3,66},{11,74},{66,3},{74,11},{5,68},{... | collective-permute-start | bytes 835592 | tf_op jit(solution)/shard_map/ppermute | solution.py:242
  50.6 14.0 %collective-permute-start.2 = (f32[136,512]{1,0:T(8,128)S(1)}, f32[136,512]{1,0:T(8,128)S(1)}, u32[]{:S(2)}, u32[]{:S(2)}) collective-permute-start(f32[136,512]{1,0:T(8,128)S(1)} %get-tuple-element.18), channel_id=1, source_target_pairs={{0,8},{1,72},{8,0},{9,64},{64,9},{65,73},{72,1},{73,65},{2,10},{3,... | collective-permute-start | bytes 835592 | tf_op jit(solution)/shard_map/ppermute | solution.py:242
  64.9 17.7 %collective-permute-start.7 = (f32[392,256]{1,0:T(8,128)S(1)}, f32[392,256]{1,0:T(8,128)S(1)}, u32[]{:S(2)}, u32[]{:S(2)}) collective-permute-start(f32[392,256]{1,0:T(8,128)S(1)} %get-tuple-element.25), channel_id=1, source_target_pairs={{0,1},{1,0},{2,3},{3,2},{4,5},{5,4},{6,7},{7,6},{8,9},{9,8},{10,11... | collective-permute-start | bytes 1204232 | tf_op jit(solution)/shard_map/ppermute | solution.py:232
  68.2 14.3 %collective-permute-start.10 = (f32[136,256]{1,0:T(8,128)S(1)}, f32[136,256]{1,0:T(8,128)S(1)}, u32[]{:S(2)}, u32[]{:S(2)}) collective-permute-start(f32[136,256]{1,0:T(8,128)S(1)} %get-tuple-element.27), channel_id=1, source_target_pairs={{0,2},{1,67},{2,4},{3,69},{4,7},{5,70},{6,1},{7,64},{8,10},{9,75},... | collective-permute-start | bytes 417800 | tf_op jit(solution)/shard_map/ppermute | solution.py:252
  72.9 10.9 %collective-permute-start.11 = (f32[136,256]{1,0:T(8,128)S(1)}, f32[136,256]{1,0:T(8,128)S(1)}, u32[]{:S(2)}, u32[]{:S(2)}) collective-permute-start(f32[136,256]{1,0:T(8,128)S(1)} %get-tuple-element.28), channel_id=1, source_target_pairs={{0,14},{1,79},{2,8},{3,73},{4,74},{5,11},{6,76},{7,13},{8,6},{9,71... | collective-permute-start | bytes 417800 | tf_op jit(solution)/shard_map/ppermute | solution.py:252
  74.8 9.4 %collective-permute-start.12 = (f32[136,256]{1,0:T(8,128)S(1)}, f32[136,256]{1,0:T(8,128)S(1)}, u32[]{:S(2)}, u32[]{:S(2)}) collective-permute-start(f32[136,256]{1,0:T(8,128)S(1)} %get-tuple-element.29), channel_id=1, source_target_pairs={{0,10},{1,75},{2,12},{3,77},{4,15},{5,78},{6,9},{7,72},{8,2},{9,67... | collective-permute-start | bytes 417800 | tf_op jit(solution)/shard_map/ppermute | solution.py:252
  77.7 9.5 %collective-permute-start.9 = (f32[136,256]{1,0:T(8,128)S(1)}, f32[136,256]{1,0:T(8,128)S(1)}, u32[]{:S(2)}, u32[]{:S(2)}) collective-permute-start(f32[136,256]{1,0:T(8,128)S(1)} %get-tuple-element.26), channel_id=1, source_target_pairs={{0,6},{1,71},{2,0},{3,65},{4,66},{5,3},{6,68},{7,5},{8,14},{9,79},... | collective-permute-start | bytes 417800 | tf_op jit(solution)/shard_map/ppermute | solution.py:252

commit v3 on v2

--- a/solution.py
+++ b/solution.py
@@ -20,14 +20,18 @@
     return jax.ShapeDtypeStruct(dims, dtype)
 
 
+def split(value):
+    high = value.astype(BF16)
+    return high, (value - high.astype(F32)).astype(BF16)
+
+
 def outer(left, right):
-    return lax.dot_general(
-        left,
-        right,
-        (((0,), (0,)), ((), ())),
-        precision=lax.Precision.HIGHEST,
-        preferred_element_type=F32,
-    )
+    def product(one, two):
+        return lax.dot_general(one, two, (((0,), (0,)), ((), ())), preferred_element_type=F32)
+
+    left_high, left_low = split(left)
+    right_high, right_low = split(right)
+    return product(left_high, right_high) + (product(left_low, right_high) + product(left_high, right_low))
 
 
 def centre_kernel(x_ref, d_ref):
@@ -42,11 +46,6 @@
     high, low = split(piece.T)
     t_ref[at : at + cols, :] = high
     t_ref[at + 2 * cols : at + 3 * cols, :] = low
-
-
-def split(value):
-    high = value.astype(BF16)
-    return high, (value - high.astype(F32)).astype(BF16)
 
 
 def against(t_ref, left):
@@ -194,24 +193,37 @@
                 total = (far[0][lo : lo + 32, :] + far[1][lo : lo + 32, :]) + (
                     far[2][lo : lo + 32, :] + far[3][lo : lo + 32, :]
                 )
-            out_ref[4 * to + y1, 0:32, :] = total + shift[k, y1, y0]
-            out_ref[4 * to + y1, 32:33, :] = own_mean
-            out_ref[4 * to + y1, 33:34, :] = row_means[k]
-            out_ref[4 * to + y1, 34:40, :] = jnp.zeros((6, cols), F32)
+            total = total + shift[k, y1, y0]
+            for g in range(4):
+                out_ref[4 * to + y1, :, cols * g : cols * g + cols] = total[8 * g : 8 * g + 8, :]
+            for row, m in ((0, own_mean), (2, row_means[k])):
+                for h in range(2):
+                    out_ref[4 * to + y1, row + h : row + h + 1, 4 * cols :] = m[:, 128 * h : 128 * h + 128]
+            out_ref[4 * to + y1, 4:8, 4 * cols :] = jnp.zeros((4, 128), F32)
 
 
 def merge_all_kernel(count, in_ref, cov_ref, mean_ref, shift):
-    blocks, _, cols = in_ref.shape
-    total = in_ref[0, 0:32, :]
+    blocks = in_ref.shape[0]
+    cols = cov_ref.shape[1]
+    total = in_ref[0]
     for s in range(1, blocks):
-        total = total + in_ref[s, 0:32, :]
-    own = jnp.concatenate([in_ref[s, 32:33, :] for s in range(blocks)], axis=0)
-    other = jnp.concatenate([in_ref[s, 33:34, :] for s in range(blocks)], axis=0)
+        total = total + in_ref[s]
+
+    def means(row):
+        halves = [
+            jnp.concatenate([in_ref[s, row + h : row + h + 1, 4 * cols :] for s in range(blocks)], axis=0)
+            for h in range(2)
+        ]
+        return jnp.concatenate(halves, axis=1)
+
+    own, other = means(0), means(2)
     own_mean = jnp.sum(own, axis=0, keepdims=True) * (1.0 / blocks)
     other_mean = jnp.sum(other, axis=0, keepdims=True) * (1.0 / blocks)
     y = 2 * lax.axis_index("y1") + lax.axis_index("y0")
-    shift[...] = (outer(other - other_mean, own - own_mean) * float(count)).reshape(8, 32, cols)
-    cov_ref[...] = (total + shift[y]) / float(count * blocks - 1)
+    shift[...] = (outer(other - other_mean, own - own_mean) * float(count)).reshape(8, 4, 8, cols)
+    for g in range(4):
+        here = total[:, cols * g : cols * g + cols] + shift[y, g]
+        cov_ref[8 * g : 8 * g + 8, :] = here / float(count * blocks - 1)
     mean_ref[...] = own_mean
 
 
@@ -291,7 +303,7 @@
     recv = shifted(send, "c", 1)
     merged = call(
         functools.partial(merge_block_kernel, rows),
-        shape(16, 40, cols),
+        shape(16, 8, 4 * cols + 128),
         (keep, recv, *far),
         (pltpu.VMEM((4, 4, 2, 32, cols), F32),),
         flops=10**9,
@@ -302,7 +314,7 @@
         functools.partial(merge_all_kernel, 4 * rows),
         (shape(32, cols), shape(1, cols)),
         (merged,),
-        (pltpu.VMEM((8, 32, cols), F32),),
+        (pltpu.VMEM((8, 4, 8, cols), F32),),
         flops=10**9,
         moved=2**20,
     )

time: 125 us -> 124 us (level)
  no operation moved by 1% of the time
where the time goes in v3:
time: 124 us; the launch traced here: 123 us
  starting transfers between devices  43.7 us (35%)
  waiting for transfers between devices  36.6 us (30%)
  blocking collectives  34.4 us (28%)
  Pallas kernels  6.53 us (5%)
    all_to_all x1, blocking collectives, steps(): merged = lax.all_to_all(merged, ('z1', 'y1'), 0, 0, tiled=True)  34.4 us
    ppermute x4, waiting for transfers between devices, shifted(): lax.ppermute(piece, axis, [(i, (i + by) % size) for i in range(size)])  21.2 us
    ppermute x4, starting transfers between devices, shifted(): lax.ppermute(piece, axis, [(i, (i + by) % size) for i in range(size)])  16.7 us
    ppermute x4, starting transfers between devices, between(): return lax.ppermute(piece, ('z0', 'y0', 'x', 'c'), pairs)  14.3 us
    ppermute x4, starting transfers between devices, dealt(): return lax.ppermute(piece, ('z0', 'y0', 'c'), pairs)  12 us
    ppermute x4, waiting for transfers between devices, dealt(): return lax.ppermute(piece, ('z0', 'y0', 'c'), pairs)  10.7 us
    pallas_call x8, Pallas kernels, call(): pl.pallas_call(kernel, out_shape=outs, in_specs=[VMEM] * len(args), out_s...  6.53 us
    ppermute x4, waiting for transfers between devices, between(): return lax.ppermute(piece, ('z0', 'y0', 'x', 'c'), pairs)  4.7 us
  transfers between devices with their start and end apart: 13, of which 6 were waited for; matrix products, arithmetic and copies ran while one was open for 0% of the time, Pallas kernels for 4%

profile of v3, /device:TPU:1, one launch (start us, length us, event | category | flops | bytes accessed | tf_op | source)
XLA Modules:
  0.0 123.3 jit_solution(6759902346384430144)
XLA Ops:
  0.6 1.2 copy-done
  2.1 5.2 %collective-permute-start.3 = (f32[1032,256]{1,0:T(8,128)S(1)}, f32[1032,256]{1,0:T(8,128)S(1)}, u32[]{:S(2)}, u32[]{:S(2)}) collective-permute-start(f32[1032,256]{1,0:T(8,128)S(1)} %shard_map.30.d_ref), channel_id=1, source_target_pairs={{0,6},{2,0},{4,2},{6,4},{1,7},{3,1},{5,3},{7,5},{8,14},{10,8},{12,... | collective-permute-start | bytes 3170312 | tf_op jit(solution)/shard_map/ppermute | solution.py:244
  7.3 5.5 %collective-permute-start = (f32[1032,256]{1,0:T(8,128)S(1)}, f32[1032,256]{1,0:T(8,128)S(1)}, u32[]{:S(2)}, u32[]{:S(2)}) collective-permute-start(f32[1032,256]{1,0:T(8,128)S(1)} %shard_map.30.d_ref), channel_id=1, source_target_pairs={{0,1},{1,0},{2,3},{3,2},{4,5},{5,4},{6,7},{7,6},{8,9},{9,8},{10,11... | collective-permute-start | bytes 3170312 | tf_op jit(solution)/shard_map/ppermute | solution.py:244
  12.8 3.6 %collective-permute-start.4 = (f32[1032,256]{1,0:T(8,128)S(1)}, f32[1032,256]{1,0:T(8,128)S(1)}, u32[]{:S(2)}, u32[]{:S(2)}) collective-permute-start(f32[1032,256]{1,0:T(8,128)S(1)} %shard_map.30.d_ref), channel_id=1, source_target_pairs={{0,2},{2,4},{4,6},{6,0},{1,3},{3,5},{5,7},{7,1},{8,10},{10,12},{12... | collective-permute-start | bytes 3170312 | tf_op jit(solution)/shard_map/ppermute | solution.py:244
  16.4 10.3 %collective-permute-done.3.up_ref = f32[1032,256]{1,0:T(8,128)S(1)} collective-permute-done((f32[1032,256]{1,0:T(8,128)S(1)}, f32[1032,256]{1,0:T(8,128)S(1)}, u32[]{:S(2)}, u32[]{:S(2)}) %collective-permute-start.3) | collective-permute-done | bytes 1056800 | tf_op jit(solution)/shard_map/ppermute | solution.py:244
  27.4 1.3 %shard_map.31 = (bf16[1024,1024]{1,0:T(8,128)(2,1)S(1)}, f32[136,512]{1,0:T(8,128)S(1)}, f32[136,512]{1,0:T(8,128)S(1)}) custom-call(f32[1032,256]{1,0:T(8,128)S(1)} %shard_map.30.d_ref, f32[1032,256]{1,0:T(8,128)S(1)} %collective-permute-done.s_ref), custom_call_target="tpu_custom_call" | custom-call | flops 2000000000 | bytes 4194304 | tf_op jit(solution)/shard_map/pallas_call | solution.py:231
  28.7 1.1 shard_map.32
  29.8 10.9 %collective-permute-done.4.down_ref = f32[1032,256]{1,0:T(8,128)S(1)} collective-permute-done((f32[1032,256]{1,0:T(8,128)S(1)}, f32[1032,256]{1,0:T(8,128)S(1)}, u32[]{:S(2)}, u32[]{:S(2)}) %collective-permute-start.4) | collective-permute-done | bytes 1056800 | tf_op jit(solution)/shard_map/ppermute | solution.py:244
  40.7 1.1 shard_map.33
  41.9 2.2 %collective-permute-start.5 = (f32[264,512]{1,0:T(8,128)S(1)}, f32[264,512]{1,0:T(8,128)S(1)}, u32[]{:S(2)}, u32[]{:S(2)}) collective-permute-start(f32[264,512]{1,0:T(8,128)S(1)} %get-tuple-element.22.refs_3_), channel_id=1, source_target_pairs={{1,64},{9,72},{64,1},{72,9},{3,66},{11,74},{66,3},{74,11},{5,68},{... | collective-permute-start | bytes 1622024 | tf_op jit(solution)/shard_map/ppermute | solution.py:254
  44.0 2.9 %collective-permute-start.6 = (f32[264,512]{1,0:T(8,128)S(1)}, f32[264,512]{1,0:T(8,128)S(1)}, u32[]{:S(2)}, u32[]{:S(2)}) collective-permute-start(f32[264,512]{1,0:T(8,128)S(1)} %get-tuple-element.23), channel_id=1, source_target_pairs={{0,8},{1,72},{8,0},{9,64},{64,9},{65,73},{72,1},{73,65},{2,10},{3,... | collective-permute-start | bytes 1622024 | tf_op jit(solution)/shard_map/ppermute | solution.py:254
  47.0 3.6 %collective-permute-start.1 = (f32[136,512]{1,0:T(8,128)S(1)}, f32[136,512]{1,0:T(8,128)S(1)}, u32[]{:S(2)}, u32[]{:S(2)}) collective-permute-start(f32[136,512]{1,0:T(8,128)S(1)} %get-tuple-element.17.refs_0_), channel_id=1, source_target_pairs={{1,64},{9,72},{64,1},{72,9},{3,66},{11,74},{66,3},{74,11},{5,68},{... | collective-permute-start | bytes 835592 | tf_op jit(solution)/shard_map/ppermute | solution.py:254
  50.6 3.3 %collective-permute-start.2 = (f32[136,512]{1,0:T(8,128)S(1)}, f32[136,512]{1,0:T(8,128)S(1)}, u32[]{:S(2)}, u32[]{:S(2)}) collective-permute-start(f32[136,512]{1,0:T(8,128)S(1)} %get-tuple-element.18), channel_id=1, source_target_pairs={{0,8},{1,72},{8,0},{9,64},{64,9},{65,73},{72,1},{73,65},{2,10},{3,... | collective-permute-start | bytes 835592 | tf_op jit(solution)/shard_map/ppermute | solution.py:254
  53.9 10.7 %collective-permute-done.1.refs_1_ = f32[136,512]{1,0:T(8,128)S(1)} collective-permute-done((f32[136,512]{1,0:T(8,128)S(1)}, f32[136,512]{1,0:T(8,128)S(1)}, u32[]{:S(2)}, u32[]{:S(2)}) %collective-permute-start.1) | collective-permute-done | bytes 278560 | tf_op jit(solution)/shard_map/ppermute | solution.py:254
  64.9 2.4 %collective-permute-start.7 = (f32[392,256]{1,0:T(8,128)S(1)}, f32[392,256]{1,0:T(8,128)S(1)}, u32[]{:S(2)}, u32[]{:S(2)}) collective-permute-start(f32[392,256]{1,0:T(8,128)S(1)} %get-tuple-element.25), channel_id=1, source_target_pairs={{0,1},{1,0},{2,3},{3,2},{4,5},{5,4},{6,7},{7,6},{8,9},{9,8},{10,11... | collective-permute-start | bytes 1204232 | tf_op jit(solution)/shard_map/ppermute | solution.py:244
  67.3 0.9 shard_map.35
  68.2 4.7 %collective-permute-start.10 = (f32[136,256]{1,0:T(8,128)S(1)}, f32[136,256]{1,0:T(8,128)S(1)}, u32[]{:S(2)}, u32[]{:S(2)}) collective-permute-start(f32[136,256]{1,0:T(8,128)S(1)} %get-tuple-element.27), channel_id=1, source_target_pairs={{0,2},{1,67},{2,4},{3,69},{4,7},{5,70},{6,1},{7,64},{8,10},{9,75},... | collective-permute-start | bytes 417800 | tf_op jit(solution)/shard_map/ppermute | solution.py:264
  72.9 1.9 %collective-permute-start.11 = (f32[136,256]{1,0:T(8,128)S(1)}, f32[136,256]{1,0:T(8,128)S(1)}, u32[]{:S(2)}, u32[]{:S(2)}) collective-permute-start(f32[136,256]{1,0:T(8,128)S(1)} %get-tuple-element.28), channel_id=1, source_target_pairs={{0,14},{1,79},{2,8},{3,73},{4,74},{5,11},{6,76},{7,13},{8,6},{9,71... | collective-permute-start | bytes 417800 | tf_op jit(solution)/shard_map/ppermute | solution.py:264
  74.8 2.9 %collective-permute-start.12 = (f32[136,256]{1,0:T(8,128)S(1)}, f32[136,256]{1,0:T(8,128)S(1)}, u32[]{:S(2)}, u32[]{:S(2)}) collective-permute-start(f32[136,256]{1,0:T(8,128)S(1)} %get-tuple-element.29), channel_id=1, source_target_pairs={{0,10},{1,75},{2,12},{3,77},{4,15},{5,78},{6,9},{7,72},{8,2},{9,67... | collective-permute-start | bytes 417800 | tf_op jit(solution)/shard_map/ppermute | solution.py:264
  77.7 4.8 %collective-permute-start.9 = (f32[136,256]{1,0:T(8,128)S(1)}, f32[136,256]{1,0:T(8,128)S(1)}, u32[]{:S(2)}, u32[]{:S(2)}) collective-permute-start(f32[136,256]{1,0:T(8,128)S(1)} %get-tuple-element.26), channel_id=1, source_target_pairs={{0,6},{1,71},{2,0},{3,65},{4,66},{5,3},{6,68},{7,5},{8,14},{9,79},... | collective-permute-start | bytes 417800 | tf_op jit(solution)/shard_map/ppermute | solution.py:264
  82.5 1.3 %collective-permute-done.11.refs_2_ = f32[136,256]{1,0:T(8,128)S(1)} collective-permute-done((f32[136,256]{1,0:T(8,128)S(1)}, f32[136,256]{1,0:T(8,128)S(1)}, u32[]{:S(2)}, u32[]{:S(2)}) %collective-permute-start.11) | collective-permute-done | bytes 139296 | tf_op jit(solution)/shard_map/ppermute | solution.py:264
  84.2 3.1 %collective-permute-done.9.refs_0_ = f32[136,256]{1,0:T(8,128)S(1)} collective-permute-done((f32[136,256]{1,0:T(8,128)S(1)}, f32[136,256]{1,0:T(8,128)S(1)}, u32[]{:S(2)}, u32[]{:S(2)}) %collective-permute-start.9) | collective-permute-done | bytes 139296 | tf_op jit(solution)/shard_map/ppermute | solution.py:264
  88.0 34.4 %all_to_all.5.in_ref = f32[16,8,1152]{2,1,0:T(8,128)S(1)} all-to-all(f32[16,8,1152]{2,1,0:T(8,128)S(1)} %shard_map.36), channel_id=1, replica_groups=mesh['z1'=4,'z0'=2,'y1'=4,'y0'=2,'x'=4,'c'=2] {'z1','y1'}, dimensions={0} | all-to-all | bytes 1179648 | tf_op jit(solution)/shard_map/all_to_all | solution.py:312
  122.4 0.9 shard_map.37
  (13 shorter events, 2.3 us)
Async XLA Ops:
  0.6 1.2 copy-start
  2.1 24.6 %collective-permute-start.3 = (f32[1032,256]{1,0:T(8,128)S(1)}, f32[1032,256]{1,0:T(8,128)S(1)}, u32[]{:S(2)}, u32[]{:S(2)}) collective-permute-start(f32[1032,256]{1,0:T(8,128)S(1)} %shard_map.30.d_ref), channel_id=1, source_target_pairs={{0,6},{2,0},{4,2},{6,4},{1,7},{3,1},{5,3},{7,5},{8,14},{10,8},{12,... | collective-permute-start | bytes 3170312 | tf_op jit(solution)/shard_map/ppermute | solution.py:244
  7.3 20.1 %collective-permute-start = (f32[1032,256]{1,0:T(8,128)S(1)}, f32[1032,256]{1,0:T(8,128)S(1)}, u32[]{:S(2)}, u32[]{:S(2)}) collective-permute-start(f32[1032,256]{1,0:T(8,128)S(1)} %shard_map.30.d_ref), channel_id=1, source_target_pairs={{0,1},{1,0},{2,3},{3,2},{4,5},{5,4},{6,7},{7,6},{8,9},{9,8},{10,11... | collective-permute-start | bytes 3170312 | tf_op jit(solution)/shard_map/ppermute | solution.py:244
  12.8 28.0 %collective-permute-start.4 = (f32[1032,256]{1,0:T(8,128)S(1)}, f32[1032,256]{1,0:T(8,128)S(1)}, u32[]{:S(2)}, u32[]{:S(2)}) collective-permute-start(f32[1032,256]{1,0:T(8,128)S(1)} %shard_map.30.d_ref), channel_id=1, source_target_pairs={{0,2},{2,4},{4,6},{6,0},{1,3},{3,5},{5,7},{7,1},{8,10},{10,12},{12... | collective-permute-start | bytes 3170312 | tf_op jit(solution)/shard_map/ppermute | solution.py:244
  26.7 40.6 %collective-permute-start.8 = (f32[1032,256]{1,0:T(8,128)S(1)}, f32[1032,256]{1,0:T(8,128)S(1)}, u32[]{:S(2)}, u32[]{:S(2)}) collective-permute-start(f32[1032,256]{1,0:T(8,128)S(1)} %collective-permute-done.3.up_ref), channel_id=1, source_target_pairs={{4,5},{5,4},{6,7},{7,6},{12,13},{13,12},{14,15},{15,14},{20,21},{2... | collective-permute-start | bytes 3170312 | tf_op jit(solution)/shard_map/ppermute | solution.py:268
  41.9 22.7 %collective-permute-start.5 = (f32[264,512]{1,0:T(8,128)S(1)}, f32[264,512]{1,0:T(8,128)S(1)}, u32[]{:S(2)}, u32[]{:S(2)}) collective-permute-start(f32[264,512]{1,0:T(8,128)S(1)} %get-tuple-element.22.refs_3_), channel_id=1, source_target_pairs={{1,64},{9,72},{64,1},{72,9},{3,66},{11,74},{66,3},{74,11},{5,68},{... | collective-permute-start | bytes 1622024 | tf_op jit(solution)/shard_map/ppermute | solution.py:254
  44.0 20.6 %collective-permute-start.6 = (f32[264,512]{1,0:T(8,128)S(1)}, f32[264,512]{1,0:T(8,128)S(1)}, u32[]{:S(2)}, u32[]{:S(2)}) collective-permute-start(f32[264,512]{1,0:T(8,128)S(1)} %get-tuple-element.23), channel_id=1, source_target_pairs={{0,8},{1,72},{8,0},{9,64},{64,9},{65,73},{72,1},{73,65},{2,10},{3,... | collective-permute-start | bytes 1622024 | tf_op jit(solution)/shard_map/ppermute | solution.py:254
  47.0 17.6 %collective-permute-start.1 = (f32[136,512]{1,0:T(8,128)S(1)}, f32[136,512]{1,0:T(8,128)S(1)}, u32[]{:S(2)}, u32[]{:S(2)}) collective-permute-start(f32[136,512]{1,0:T(8,128)S(1)} %get-tuple-element.17.refs_0_), channel_id=1, source_target_pairs={{1,64},{9,72},{64,1},{72,9},{3,66},{11,74},{66,3},{74,11},{5,68},{... | collective-permute-start | bytes 835592 | tf_op jit(solution)/shard_map/ppermute | solution.py:254
  50.6 14.0 %collective-permute-start.2 = (f32[136,512]{1,0:T(8,128)S(1)}, f32[136,512]{1,0:T(8,128)S(1)}, u32[]{:S(2)}, u32[]{:S(2)}) collective-permute-start(f32[136,512]{1,0:T(8,128)S(1)} %get-tuple-element.18), channel_id=1, source_target_pairs={{0,8},{1,72},{8,0},{9,64},{64,9},{65,73},{72,1},{73,65},{2,10},{3,... | collective-permute-start | bytes 835592 | tf_op jit(solution)/shard_map/ppermute | solution.py:254
  64.9 17.7 %collective-permute-start.7 = (f32[392,256]{1,0:T(8,128)S(1)}, f32[392,256]{1,0:T(8,128)S(1)}, u32[]{:S(2)}, u32[]{:S(2)}) collective-permute-start(f32[392,256]{1,0:T(8,128)S(1)} %get-tuple-element.25), channel_id=1, source_target_pairs={{0,1},{1,0},{2,3},{3,2},{4,5},{5,4},{6,7},{7,6},{8,9},{9,8},{10,11... | collective-permute-start | bytes 1204232 | tf_op jit(solution)/shard_map/ppermute | solution.py:244
  68.2 14.3 %collective-permute-start.10 = (f32[136,256]{1,0:T(8,128)S(1)}, f32[136,256]{1,0:T(8,128)S(1)}, u32[]{:S(2)}, u32[]{:S(2)}) collective-permute-start(f32[136,256]{1,0:T(8,128)S(1)} %get-tuple-element.27), channel_id=1, source_target_pairs={{0,2},{1,67},{2,4},{3,69},{4,7},{5,70},{6,1},{7,64},{8,10},{9,75},... | collective-permute-start | bytes 417800 | tf_op jit(solution)/shard_map/ppermute | solution.py:264
  72.9 10.9 %collective-permute-start.11 = (f32[136,256]{1,0:T(8,128)S(1)}, f32[136,256]{1,0:T(8,128)S(1)}, u32[]{:S(2)}, u32[]{:S(2)}) collective-permute-start(f32[136,256]{1,0:T(8,128)S(1)} %get-tuple-element.28), channel_id=1, source_target_pairs={{0,14},{1,79},{2,8},{3,73},{4,74},{5,11},{6,76},{7,13},{8,6},{9,71... | collective-permute-start | bytes 417800 | tf_op jit(solution)/shard_map/ppermute | solution.py:264
  74.8 9.4 %collective-permute-start.12 = (f32[136,256]{1,0:T(8,128)S(1)}, f32[136,256]{1,0:T(8,128)S(1)}, u32[]{:S(2)}, u32[]{:S(2)}) collective-permute-start(f32[136,256]{1,0:T(8,128)S(1)} %get-tuple-element.29), channel_id=1, source_target_pairs={{0,10},{1,75},{2,12},{3,77},{4,15},{5,78},{6,9},{7,72},{8,2},{9,67... | collective-permute-start | bytes 417800 | tf_op jit(solution)/shard_map/ppermute | solution.py:264
  77.7 9.5 %collective-permute-start.9 = (f32[136,256]{1,0:T(8,128)S(1)}, f32[136,256]{1,0:T(8,128)S(1)}, u32[]{:S(2)}, u32[]{:S(2)}) collective-permute-start(f32[136,256]{1,0:T(8,128)S(1)} %get-tuple-element.26), channel_id=1, source_target_pairs={{0,6},{1,71},{2,0},{3,65},{4,66},{5,3},{6,68},{7,5},{8,14},{9,79},... | collective-permute-start | bytes 417800 | tf_op jit(solution)/shard_map/ppermute | solution.py:264

commit v4 on v3

--- a/solution.py
+++ b/solution.py
@@ -107,7 +107,7 @@
     outs, (block, mean) = refs[:4], refs[4:]
     rows, cols = up_ref.shape[0] - 8, up_ref.shape[1]
     z0, y0 = lax.axis_index("z0"), lax.axis_index("y0")
-    crossed = jnp.full((1, cols), lax.axis_index("x") >= 2)
+    crossed = jnp.full((1, cols), lax.axis_index("x") < 2)
     above = jnp.where(crossed, cross_ref[...], up_ref[...])
     high, low = split(above[0:rows].T)
     right_high, right_low = split(down_ref[0:rows, :])
@@ -258,14 +258,14 @@
     pairs = []
     for i in range(32):
         z0, y0, x, c = i // 16, i // 8 % 2, i // 2 % 4, i % 2
-        above = 1 - c if x >= 2 else c
+        above = 1 - c if x < 2 else c
         x_to, z_to, c_to = ((x + 1) % 4, c, above) if z0 ^ s else ((x + 3) % 4, above, c)
         pairs.append((i, z_to * 16 + (y0 ^ dy) * 8 + x_to * 2 + c_to))
     return lax.ppermute(piece, ("z0", "y0", "x", "c"), pairs)
 
 
 def crossed(piece):
-    return lax.ppermute(piece, ("x", "c"), [(4, 5), (5, 4), (6, 7), (7, 6)])
+    return lax.ppermute(piece, ("x", "c"), [(0, 1), (1, 0), (2, 3), (3, 2)])
 
 
 def steps(x):

time: 124 us -> 123 us (level)
  the two profiles are of different devices: /device:TPU:1 before, /device:TPU:8 now
where the time goes in v4:
time: 123 us; the launch traced here: 122 us
  waiting for transfers between devices  43.6 us (35%)
  blocking collectives  35.3 us (29%)
  starting transfers between devices  34.8 us (28%)
  Pallas kernels  6.56 us (5%)
    all_to_all x1, blocking collectives, steps(): merged = lax.all_to_all(merged, ('z1', 'y1'), 0, 0, tiled=True)  35.3 us
    ppermute x4, waiting for transfers between devices, shifted(): lax.ppermute(piece, axis, [(i, (i + by) % size) for i in range(size)])  22.6 us
    ppermute x4, waiting for transfers between devices, dealt(): return lax.ppermute(piece, ('z0', 'y0', 'c'), pairs)  15 us
    ppermute x4, starting transfers between devices, between(): return lax.ppermute(piece, ('z0', 'y0', 'x', 'c'), pairs)  13.2 us
    ppermute x4, starting transfers between devices, shifted(): lax.ppermute(piece, axis, [(i, (i + by) % size) for i in range(size)])  11.5 us
    ppermute x4, starting transfers between devices, dealt(): return lax.ppermute(piece, ('z0', 'y0', 'c'), pairs)  8.25 us
    pallas_call x8, Pallas kernels, call(): pl.pallas_call(kernel, out_shape=outs, in_specs=[VMEM] * len(args), out_s...  6.56 us
    ppermute x4, waiting for transfers between devices, between(): return lax.ppermute(piece, ('z0', 'y0', 'x', 'c'), pairs)  6.02 us
  transfers between devices with their start and end apart: 13, of which 5 were waited for; matrix products, arithmetic and copies ran while one was open for 0% of the time, Pallas kernels for 4%

profile of v4, /device:TPU:8, one launch (start us, length us, event | category | flops | bytes accessed | tf_op | source)
XLA Modules:
  0.0 122.4 jit_solution(7133792002576083298)
XLA Ops:
  0.6 1.2 copy-done
  2.1 4.7 %collective-permute-start.3 = (f32[1032,256]{1,0:T(8,128)S(1)}, f32[1032,256]{1,0:T(8,128)S(1)}, u32[]{:S(2)}, u32[]{:S(2)}) collective-permute-start(f32[1032,256]{1,0:T(8,128)S(1)} %shard_map.30.d_ref), channel_id=1, source_target_pairs={{0,6},{2,0},{4,2},{6,4},{1,7},{3,1},{5,3},{7,5},{8,14},{10,8},{12,... | collective-permute-start | bytes 3170312 | tf_op jit(solution)/shard_map/ppermute | solution.py:244
  6.7 1.9 %collective-permute-start = (f32[1032,256]{1,0:T(8,128)S(1)}, f32[1032,256]{1,0:T(8,128)S(1)}, u32[]{:S(2)}, u32[]{:S(2)}) collective-permute-start(f32[1032,256]{1,0:T(8,128)S(1)} %shard_map.30.d_ref), channel_id=1, source_target_pairs={{0,1},{1,0},{2,3},{3,2},{4,5},{5,4},{6,7},{7,6},{8,9},{9,8},{10,11... | collective-permute-start | bytes 3170312 | tf_op jit(solution)/shard_map/ppermute | solution.py:244
  8.7 1.9 %collective-permute-start.4 = (f32[1032,256]{1,0:T(8,128)S(1)}, f32[1032,256]{1,0:T(8,128)S(1)}, u32[]{:S(2)}, u32[]{:S(2)}) collective-permute-start(f32[1032,256]{1,0:T(8,128)S(1)} %shard_map.30.d_ref), channel_id=1, source_target_pairs={{0,2},{2,4},{4,6},{6,0},{1,3},{3,5},{5,7},{7,1},{8,10},{10,12},{12... | collective-permute-start | bytes 3170312 | tf_op jit(solution)/shard_map/ppermute | solution.py:244
  10.6 18.7 %collective-permute-done.3.up_ref = f32[1032,256]{1,0:T(8,128)S(1)} collective-permute-done((f32[1032,256]{1,0:T(8,128)S(1)}, f32[1032,256]{1,0:T(8,128)S(1)}, u32[]{:S(2)}, u32[]{:S(2)}) %collective-permute-start.3) | collective-permute-done | bytes 1056800 | tf_op jit(solution)/shard_map/ppermute | solution.py:244
  29.3 1.9 %collective-permute-start.8 = (f32[1032,256]{1,0:T(8,128)S(1)}, f32[1032,256]{1,0:T(8,128)S(1)}, u32[]{:S(2)}, u32[]{:S(2)}) collective-permute-start(f32[1032,256]{1,0:T(8,128)S(1)} %collective-permute-done.3.up_ref), channel_id=1, source_target_pairs={{0,1},{1,0},{2,3},{3,2},{8,9},{9,8},{10,11},{11,10},{16,17},{17,16... | collective-permute-start | bytes 3170312 | tf_op jit(solution)/shard_map/ppermute | solution.py:268
  31.2 1.3 %shard_map.31 = (bf16[1024,1024]{1,0:T(8,128)(2,1)S(1)}, f32[136,512]{1,0:T(8,128)S(1)}, f32[136,512]{1,0:T(8,128)S(1)}) custom-call(f32[1032,256]{1,0:T(8,128)S(1)} %shard_map.30.d_ref, f32[1032,256]{1,0:T(8,128)S(1)} %collective-permute-done.s_ref), custom_call_target="tpu_custom_call" | custom-call | flops 2000000000 | bytes 4194304 | tf_op jit(solution)/shard_map/pallas_call | solution.py:231
  32.5 1.1 shard_map.32
  33.6 3.9 %collective-permute-done.4.down_ref = f32[1032,256]{1,0:T(8,128)S(1)} collective-permute-done((f32[1032,256]{1,0:T(8,128)S(1)}, f32[1032,256]{1,0:T(8,128)S(1)}, u32[]{:S(2)}, u32[]{:S(2)}) %collective-permute-start.4) | collective-permute-done | bytes 1056800 | tf_op jit(solution)/shard_map/ppermute | solution.py:244
  37.5 1.1 shard_map.33
  39.3 5.0 %collective-permute-start.6 = (f32[264,512]{1,0:T(8,128)S(1)}, f32[264,512]{1,0:T(8,128)S(1)}, u32[]{:S(2)}, u32[]{:S(2)}) collective-permute-start(f32[264,512]{1,0:T(8,128)S(1)} %get-tuple-element.23), channel_id=1, source_target_pairs={{0,8},{1,72},{8,0},{9,64},{64,9},{65,73},{72,1},{73,65},{2,10},{3,... | collective-permute-start | bytes 1622024 | tf_op jit(solution)/shard_map/ppermute | solution.py:254
  45.0 1.9 %collective-permute-start.2 = (f32[136,512]{1,0:T(8,128)S(1)}, f32[136,512]{1,0:T(8,128)S(1)}, u32[]{:S(2)}, u32[]{:S(2)}) collective-permute-start(f32[136,512]{1,0:T(8,128)S(1)} %get-tuple-element.18), channel_id=1, source_target_pairs={{0,8},{1,72},{8,0},{9,64},{64,9},{65,73},{72,1},{73,65},{2,10},{3,... | collective-permute-start | bytes 835592 | tf_op jit(solution)/shard_map/ppermute | solution.py:254
  46.9 15.0 %collective-permute-done.2.refs_2_ = f32[136,512]{1,0:T(8,128)S(1)} collective-permute-done((f32[136,512]{1,0:T(8,128)S(1)}, f32[136,512]{1,0:T(8,128)S(1)}, u32[]{:S(2)}, u32[]{:S(2)}) %collective-permute-start.2) | collective-permute-done | bytes 278560 | tf_op jit(solution)/shard_map/ppermute | solution.py:254
  62.2 3.0 %collective-permute-start.7 = (f32[392,256]{1,0:T(8,128)S(1)}, f32[392,256]{1,0:T(8,128)S(1)}, u32[]{:S(2)}, u32[]{:S(2)}) collective-permute-start(f32[392,256]{1,0:T(8,128)S(1)} %get-tuple-element.25), channel_id=1, source_target_pairs={{0,1},{1,0},{2,3},{3,2},{4,5},{5,4},{6,7},{7,6},{8,9},{9,8},{10,11... | collective-permute-start | bytes 1204232 | tf_op jit(solution)/shard_map/ppermute | solution.py:244
  65.2 0.9 shard_map.35
  66.1 3.0 %collective-permute-start.10 = (f32[136,256]{1,0:T(8,128)S(1)}, f32[136,256]{1,0:T(8,128)S(1)}, u32[]{:S(2)}, u32[]{:S(2)}) collective-permute-start(f32[136,256]{1,0:T(8,128)S(1)} %get-tuple-element.27), channel_id=1, source_target_pairs={{0,3},{1,66},{2,5},{3,68},{4,6},{5,71},{6,0},{7,65},{8,11},{9,74},... | collective-permute-start | bytes 417800 | tf_op jit(solution)/shard_map/ppermute | solution.py:264
  69.1 3.9 %collective-permute-start.11 = (f32[136,256]{1,0:T(8,128)S(1)}, f32[136,256]{1,0:T(8,128)S(1)}, u32[]{:S(2)}, u32[]{:S(2)}) collective-permute-start(f32[136,256]{1,0:T(8,128)S(1)} %get-tuple-element.28), channel_id=1, source_target_pairs={{0,78},{1,15},{2,72},{3,9},{4,10},{5,75},{6,12},{7,77},{8,70},{9,7... | collective-permute-start | bytes 417800 | tf_op jit(solution)/shard_map/ppermute | solution.py:264
  73.0 3.3 %collective-permute-start.12 = (f32[136,256]{1,0:T(8,128)S(1)}, f32[136,256]{1,0:T(8,128)S(1)}, u32[]{:S(2)}, u32[]{:S(2)}) collective-permute-start(f32[136,256]{1,0:T(8,128)S(1)} %get-tuple-element.29), channel_id=1, source_target_pairs={{0,11},{1,74},{2,13},{3,76},{4,14},{5,79},{6,8},{7,73},{8,3},{9,66... | collective-permute-start | bytes 417800 | tf_op jit(solution)/shard_map/ppermute | solution.py:264
  76.3 3.0 %collective-permute-start.9 = (f32[136,256]{1,0:T(8,128)S(1)}, f32[136,256]{1,0:T(8,128)S(1)}, u32[]{:S(2)}, u32[]{:S(2)}) collective-permute-start(f32[136,256]{1,0:T(8,128)S(1)} %get-tuple-element.26), channel_id=1, source_target_pairs={{0,70},{1,7},{2,64},{3,1},{4,2},{5,67},{6,4},{7,69},{8,78},{9,15},... | collective-permute-start | bytes 417800 | tf_op jit(solution)/shard_map/ppermute | solution.py:264
  79.4 3.3 %collective-permute-done.12.refs_3_ = f32[136,256]{1,0:T(8,128)S(1)} collective-permute-done((f32[136,256]{1,0:T(8,128)S(1)}, f32[136,256]{1,0:T(8,128)S(1)}, u32[]{:S(2)}, u32[]{:S(2)}) %collective-permute-start.12) | collective-permute-done | bytes 139296 | tf_op jit(solution)/shard_map/ppermute | solution.py:264
  82.7 2.6 %collective-permute-done.9.refs_0_ = f32[136,256]{1,0:T(8,128)S(1)} collective-permute-done((f32[136,256]{1,0:T(8,128)S(1)}, f32[136,256]{1,0:T(8,128)S(1)}, u32[]{:S(2)}, u32[]{:S(2)}) %collective-permute-start.9) | collective-permute-done | bytes 139296 | tf_op jit(solution)/shard_map/ppermute | solution.py:264
  85.4 0.8 shard_map.36
  86.1 35.3 %all_to_all.5.in_ref = f32[16,8,1152]{2,1,0:T(8,128)S(1)} all-to-all(f32[16,8,1152]{2,1,0:T(8,128)S(1)} %shard_map.36), channel_id=1, replica_groups=mesh['z1'=4,'z0'=2,'y1'=4,'y0'=2,'x'=4,'c'=2] {'z1','y1'}, dimensions={0} | all-to-all | bytes 1179648 | tf_op jit(solution)/shard_map/all_to_all | solution.py:312
  121.4 0.9 shard_map.37
  (13 shorter events, 1.9 us)
Async XLA Ops:
  0.6 1.2 %copy-start = (f32[1024,256]{1,0:T(8,128)S(1)}, f32[1024,256]{1,0:T(8,128)}, u32[]{:S(2)}) copy-start(f32[1024,256]{1,0:T(8,128)} %x_ref.1) | copy-start | bytes 3145732
  2.1 27.2 %collective-permute-start.3 = (f32[1032,256]{1,0:T(8,128)S(1)}, f32[1032,256]{1,0:T(8,128)S(1)}, u32[]{:S(2)}, u32[]{:S(2)}) collective-permute-start(f32[1032,256]{1,0:T(8,128)S(1)} %shard_map.30.d_ref), channel_id=1, source_target_pairs={{0,6},{2,0},{4,2},{6,4},{1,7},{3,1},{5,3},{7,5},{8,14},{10,8},{12,... | collective-permute-start | bytes 3170312 | tf_op jit(solution)/shard_map/ppermute | solution.py:244
  6.7 24.5 %collective-permute-start = (f32[1032,256]{1,0:T(8,128)S(1)}, f32[1032,256]{1,0:T(8,128)S(1)}, u32[]{:S(2)}, u32[]{:S(2)}) collective-permute-start(f32[1032,256]{1,0:T(8,128)S(1)} %shard_map.30.d_ref), channel_id=1, source_target_pairs={{0,1},{1,0},{2,3},{3,2},{4,5},{5,4},{6,7},{7,6},{8,9},{9,8},{10,11... | collective-permute-start | bytes 3170312 | tf_op jit(solution)/shard_map/ppermute | solution.py:244
  8.7 28.8 %collective-permute-start.4 = (f32[1032,256]{1,0:T(8,128)S(1)}, f32[1032,256]{1,0:T(8,128)S(1)}, u32[]{:S(2)}, u32[]{:S(2)}) collective-permute-start(f32[1032,256]{1,0:T(8,128)S(1)} %shard_map.30.d_ref), channel_id=1, source_target_pairs={{0,2},{2,4},{4,6},{6,0},{1,3},{3,5},{5,7},{7,1},{8,10},{10,12},{12... | collective-permute-start | bytes 3170312 | tf_op jit(solution)/shard_map/ppermute | solution.py:244
  29.3 35.9 %collective-permute-start.8 = (f32[1032,256]{1,0:T(8,128)S(1)}, f32[1032,256]{1,0:T(8,128)S(1)}, u32[]{:S(2)}, u32[]{:S(2)}) collective-permute-start(f32[1032,256]{1,0:T(8,128)S(1)} %collective-permute-done.3.up_ref), channel_id=1, source_target_pairs={{0,1},{1,0},{2,3},{3,2},{8,9},{9,8},{10,11},{11,10},{16,17},{17,16... | collective-permute-start | bytes 3170312 | tf_op jit(solution)/shard_map/ppermute | solution.py:268
  38.6 23.3 %collective-permute-start.5 = (f32[264,512]{1,0:T(8,128)S(1)}, f32[264,512]{1,0:T(8,128)S(1)}, u32[]{:S(2)}, u32[]{:S(2)}) collective-permute-start(f32[264,512]{1,0:T(8,128)S(1)} %get-tuple-element.22.refs_3_), channel_id=1, source_target_pairs={{1,64},{9,72},{64,1},{72,9},{3,66},{11,74},{66,3},{74,11},{5,68},{... | collective-permute-start | bytes 1622024 | tf_op jit(solution)/shard_map/ppermute | solution.py:254
  39.3 22.6 %collective-permute-start.6 = (f32[264,512]{1,0:T(8,128)S(1)}, f32[264,512]{1,0:T(8,128)S(1)}, u32[]{:S(2)}, u32[]{:S(2)}) collective-permute-start(f32[264,512]{1,0:T(8,128)S(1)} %get-tuple-element.23), channel_id=1, source_target_pairs={{0,8},{1,72},{8,0},{9,64},{64,9},{65,73},{72,1},{73,65},{2,10},{3,... | collective-permute-start | bytes 1622024 | tf_op jit(solution)/shard_map/ppermute | solution.py:254
  44.3 2.6 %collective-permute-start.1 = (f32[136,512]{1,0:T(8,128)S(1)}, f32[136,512]{1,0:T(8,128)S(1)}, u32[]{:S(2)}, u32[]{:S(2)}) collective-permute-start(f32[136,512]{1,0:T(8,128)S(1)} %get-tuple-element.17.refs_0_), channel_id=1, source_target_pairs={{1,64},{9,72},{64,1},{72,9},{3,66},{11,74},{66,3},{74,11},{5,68},{... | collective-permute-start | bytes 835592 | tf_op jit(solution)/shard_map/ppermute | solution.py:254
  45.0 17.0 %collective-permute-start.2 = (f32[136,512]{1,0:T(8,128)S(1)}, f32[136,512]{1,0:T(8,128)S(1)}, u32[]{:S(2)}, u32[]{:S(2)}) collective-permute-start(f32[136,512]{1,0:T(8,128)S(1)} %get-tuple-element.18), channel_id=1, source_target_pairs={{0,8},{1,72},{8,0},{9,64},{64,9},{65,73},{72,1},{73,65},{2,10},{3,... | collective-permute-start | bytes 835592 | tf_op jit(solution)/shard_map/ppermute | solution.py:254
  62.2 17.1 %collective-permute-start.7 = (f32[392,256]{1,0:T(8,128)S(1)}, f32[392,256]{1,0:T(8,128)S(1)}, u32[]{:S(2)}, u32[]{:S(2)}) collective-permute-start(f32[392,256]{1,0:T(8,128)S(1)} %get-tuple-element.25), channel_id=1, source_target_pairs={{0,1},{1,0},{2,3},{3,2},{4,5},{5,4},{6,7},{7,6},{8,9},{9,8},{10,11... | collective-permute-start | bytes 1204232 | tf_op jit(solution)/shard_map/ppermute | solution.py:244
  66.1 13.2 %collective-permute-start.10 = (f32[136,256]{1,0:T(8,128)S(1)}, f32[136,256]{1,0:T(8,128)S(1)}, u32[]{:S(2)}, u32[]{:S(2)}) collective-permute-start(f32[136,256]{1,0:T(8,128)S(1)} %get-tuple-element.27), channel_id=1, source_target_pairs={{0,3},{1,66},{2,5},{3,68},{4,6},{5,71},{6,0},{7,65},{8,11},{9,74},... | collective-permute-start | bytes 417800 | tf_op jit(solution)/shard_map/ppermute | solution.py:264
  69.1 10.3 %collective-permute-start.11 = (f32[136,256]{1,0:T(8,128)S(1)}, f32[136,256]{1,0:T(8,128)S(1)}, u32[]{:S(2)}, u32[]{:S(2)}) collective-permute-start(f32[136,256]{1,0:T(8,128)S(1)} %get-tuple-element.28), channel_id=1, source_target_pairs={{0,78},{1,15},{2,72},{3,9},{4,10},{5,75},{6,12},{7,77},{8,70},{9,7... | collective-permute-start | bytes 417800 | tf_op jit(solution)/shard_map/ppermute | solution.py:264
  73.0 9.7 %collective-permute-start.12 = (f32[136,256]{1,0:T(8,128)S(1)}, f32[136,256]{1,0:T(8,128)S(1)}, u32[]{:S(2)}, u32[]{:S(2)}) collective-permute-start(f32[136,256]{1,0:T(8,128)S(1)} %get-tuple-element.29), channel_id=1, source_target_pairs={{0,11},{1,74},{2,13},{3,76},{4,14},{5,79},{6,8},{7,73},{8,3},{9,66... | collective-permute-start | bytes 417800 | tf_op jit(solution)/shard_map/ppermute | solution.py:264
  76.3 9.1 %collective-permute-start.9 = (f32[136,256]{1,0:T(8,128)S(1)}, f32[136,256]{1,0:T(8,128)S(1)}, u32[]{:S(2)}, u32[]{:S(2)}) collective-permute-start(f32[136,256]{1,0:T(8,128)S(1)} %get-tuple-element.26), channel_id=1, source_target_pairs={{0,70},{1,7},{2,64},{3,1},{4,2},{5,67},{6,4},{7,69},{8,78},{9,15},... | collective-permute-start | bytes 417800 | tf_op jit(solution)/shard_map/ppermute | solution.py:264
